TPU v7x, 32 devices: a whole 2x2x4 slice. The times are simulated.
32 devices in a mesh: ep: 8 (over z, y), dp: 4 (over x, core).
Axes of the slice: x: 2, y: 2, z: 4, core: 2. Of those that a mesh axis runs over, the one named last changes fastest.
Arguments:
- tokens: bfloat16 [6144, 2880], P(('ep', 'dp')), may hold values from -64 to 64
- out_grad: bfloat16 [6144, 2880], P(('ep', 'dp')), may hold values from -6 to 6
- indices: int32 [6144, 4], P(('ep', 'dp')), may hold values from 0 to 31, as said below
- expert_rows: bfloat16 [4, 32, 8, 36, 2880], P('dp', 'ep'), may hold values from -0.111328125 to 0.111328125
- router_weight: bfloat16 [2880, 32], replicated, may hold values from -1 to 1
- router_bias: float32 [32], replicated, may hold values from -3 to 3
- balance_scale: float32 [1], replicated, may hold values from 64 to 256
Outputs:
- token_grad: bfloat16 [6144, 2880], P(('ep', 'dp'))
- weight_grad: float32 [2880, 32], P('dp', 'ep')
- balance_loss: float32 [1], replicated
Inputs may be any that keep to these rules, and one draw needn't show every extreme that they name: `indices`: each row names 4 different experts. Within the 192 rows of one device no expert is named by more than 36 rows, and some expert is named by exactly 36 rows. Within the rows of one device the 4 experts of one ep index (experts j * 4 to j * 4 + 3) are named by at most 108 rows together, and those of some ep index by exactly 108. Every expert is named by some row of every device.
All inputs are finite; a program needn't handle non-finite values.
Results may differ from a plain program's by a relative error of at most 0.0014.
The roundings to bfloat16 on the way count: a program that leaves them out, or rounds other values in their place, can miss the bound.
Values may be sent and summed in bfloat16 or wider, within the bound.
No kernel may reach another device: no remote copies, remote signals or barrier semaphores. Data moves between devices by JAX's collectives and lax.ppermute only.
A program may use at most 128 MiB of HBM per device.

v0:
```python
import math

import jax
import jax.numpy as jnp
from jax import lax
from jax.experimental import pallas as pl
from jax.experimental.pallas import tpu as pltpu
from jax.sharding import PartitionSpec as P


F32, BF16 = jnp.float32, jnp.bfloat16


NT = (((1,), (1,)), ((), ()))
ANYWHERE = pl.BlockSpec(memory_space=pl.ANY)
SCALARS = pl.BlockSpec(memory_space=pltpu.SMEM)
LOCAL = pl.BlockSpec(memory_space=pltpu.VMEM)


def spot(length):
    me = lax.axis_index("ep")
    side, place = lax.rem(me, 2), lax.div(me, 2)
    return side, place, place < length - length // 2


def source_at(length, n):
    _, place, low = spot(length)
    ahead = place + jnp.where(low, length - 1 - n, n + 1)
    return jnp.where(ahead >= length, ahead - length, ahead)


def split_rows(table, wanted, ep):
    total, width = table.shape
    count, entries = len(wanted), total // ep
    rows = 16 if entries % 16 == 0 else entries
    block_in, parts = rows * ep, entries // rows
    group = max(g for g in (1, 2, 3) if parts % g == 0)

    def body(x_ref, *refs):
        outs, sel_ref = refs[:count], refs[count]

        @pl.when(pl.program_id(0) == 0)
        def _():
            side, _, _ = spot(ep // 2)
            row = lax.broadcasted_iota(jnp.int32, (rows, block_in), 0)
            column = lax.broadcasted_iota(jnp.int32, (rows, block_in), 1)
            for k, (n, across) in enumerate(wanted):
                source = 2 * source_at(ep // 2, n) + (1 - side if across else side)
                sel_ref[k * rows:(k + 1) * rows, :] = (column == row * ep + source).astype(F32).astype(BF16)

        for k in range(group):
            x = x_ref[k * block_in:(k + 1) * block_in, :]
            y = jnp.dot(sel_ref[...], x, preferred_element_type=F32).astype(BF16)
            for c in range(count):
                outs[c][k * rows:(k + 1) * rows, :] = y[c * rows:(c + 1) * rows]

    return pl.pallas_call(
        body,
        grid=(parts // group,),
        in_specs=[pl.BlockSpec((group * block_in, width), lambda i: (i, 0))],
        out_specs=[pl.BlockSpec((group * rows, width), lambda i: (i, 0))] * count,
        out_shape=[jax.ShapeDtypeStruct((entries, width), BF16)] * count,
        scratch_shapes=[pltpu.VMEM((count * rows, block_in), BF16)],
        cost_estimate=pl.CostEstimate(
            flops=2 * count * rows * block_in * width * parts, bytes_accessed=3 * total * width, transcendentals=0
        ),
        name="split_rows",
    )(table)


def slot_marks(chosen, ep, exp_dev):
    tok = chosen.shape[1]
    experts = ep * exp_dev

    def body(chosen_ref, out_ref):
        ids = lax.broadcasted_iota(jnp.int32, (experts, tok), 0)
        named = jnp.zeros((experts, tok), jnp.bool_)
        for k in range(chosen.shape[0]):
            named = named | (ids == chosen_ref[k:k + 1, :])
        earlier = lax.broadcasted_iota(jnp.int32, (tok, tok), 0) < lax.broadcasted_iota(jnp.int32, (tok, tok), 1)
        before = jnp.dot(
            named.astype(F32).astype(BF16), earlier.astype(F32).astype(BF16), preferred_element_type=F32
        )
        marks = jnp.where(named, before.astype(jnp.int32), -1)
        for j in range(ep):
            out_ref[:, j] = jnp.broadcast_to(marks[None, j * exp_dev:(j + 1) * exp_dev], (ep, exp_dev, tok))

    return pl.pallas_call(
        body,
        in_specs=[LOCAL],
        out_specs=LOCAL,
        out_shape=jax.ShapeDtypeStruct((ep, ep, exp_dev, tok), jnp.int32),
        cost_estimate=pl.CostEstimate(flops=2 * experts * tok * tok, bytes_accessed=4 * ep * experts * tok, transcendentals=0),
        name="slot_marks",
    )(chosen)


def router(weight, tokens, bias, marks):
    experts, tok = weight.shape[0], tokens.shape[0]

    def body(weight_ref, tokens_ref, bias_ref, marks_ref, probability_ref, mix_ref, sums_ref):
        logits = lax.dot_general(weight_ref[...], tokens_ref[...], NT, preferred_element_type=F32) + bias_ref[...]
        powers = jnp.exp(logits - jnp.max(logits, axis=0, keepdims=True))
        probability = powers / jnp.sum(powers, axis=0, keepdims=True)
        probability_ref[...] = probability
        named = jnp.concatenate([marks_ref[j] for j in range(marks.shape[0])], axis=0) >= 0
        best = jnp.max(jnp.where(named, logits, -jnp.inf), axis=0, keepdims=True)
        powers = jnp.where(named, jnp.exp(jnp.where(named, logits, best) - best), 0.0)
        mix_ref[...] = powers / jnp.sum(powers, axis=0, keepdims=True)
        square = (experts, experts)
        same = lax.broadcasted_iota(jnp.int32, square, 0) == lax.broadcasted_iota(jnp.int32, square, 1)
        sums = jnp.where(same, jnp.sum(probability, axis=1, keepdims=True), 0.0)
        sums_ref[...] = jnp.sum(sums, axis=0, keepdims=True)

    return pl.pallas_call(
        body,
        in_specs=[LOCAL] * 4,
        out_specs=[LOCAL] * 3,
        out_shape=[jax.ShapeDtypeStruct((experts, tok), F32)] * 2 + [jax.ShapeDtypeStruct((1, experts), F32)],
        cost_estimate=pl.CostEstimate(
            flops=2 * experts * tok * weight.shape[1], bytes_accessed=2 * (weight.size + tokens.size), transcendentals=2 * experts * tok
        ),
        name="router",
    )(weight, tokens, bias, marks)


def slot_dots(rows, block, marks, exp_dev, put):
    kinds, count, width = rows.shape
    tok, cap = block.shape[0], count // exp_dev
    if count % 16 == 0:
        full = lax.dot_general(rows[...].reshape(kinds * count, width), block[...], NT, preferred_element_type=F32)
        full = [full[k * count:(k + 1) * count] for k in range(kinds)]
    else:
        full = [lax.dot_general(rows[k], block[...], NT, preferred_element_type=F32) for k in range(kinds)]
    slots = lax.broadcasted_iota(jnp.int32, (cap, tok), 0)
    for kind, mark in enumerate(marks):
        for e in range(exp_dev):
            part = jnp.where(slots == mark[e:e + 1], full[kind][e * cap:(e + 1) * cap], 0.0)
            put(kind, e, jnp.sum(part, axis=0, keepdims=True))


def meet(blocks, jobs, marks, message, exp_dev):
    tok, width = blocks[0].shape
    length = message.shape[0]
    flat = [r for job in jobs for r in job[0]]
    count = flat[0].shape[0]
    most = max(len(job[0]) for job in jobs)
    first = [sum(len(job[0]) for job in jobs[:n]) for n in range(len(jobs))]

    def body(*refs):
        block_refs, refs = refs[:len(blocks)], refs[len(blocks):]
        row_refs, refs = refs[:len(flat)], refs[len(flat):]
        marks_ref, in_ref, out_ref, held, rows_held, block_sem, row_sem = refs
        side = spot(length)[0]
        plans = [job[2]() for job in jobs]

        def usable(n):
            return (plans[n][2] >= 0) & (plans[n][2] < len(blocks))

        def rows_copy(n, k):
            return pltpu.make_async_copy(row_refs[first[n] + k], rows_held.at[n % 2, k], row_sem.at[n % 2, k])

        def start(n):
            for i, block in enumerate(block_refs):
                @pl.when(plans[n][2] == i)
                def _(block=block):
                    pltpu.make_async_copy(block, held.at[n % 2], block_sem.at[n % 2]).start()

            @pl.when(usable(n))
            def _():
                for k in range(len(jobs[n][0])):
                    rows_copy(n, k).start()

        start(0)
        out_ref[...] = in_ref[...]
        for n in range(len(jobs)):
            if n + 1 < len(jobs):
                start(n + 1)

            @pl.when(usable(n))
            def _(n=n):
                pltpu.make_async_copy(block_refs[0], held.at[n % 2], block_sem.at[n % 2]).wait()
                rows, kinds = jobs[n][:2]
                source, column, _ = plans[n]
                for k in range(len(rows)):
                    rows_copy(n, k).wait()

                def put(k, e, value):
                    line = jobs[n][3] + kinds[k] * exp_dev + e
                    out_ref[pl.ds(source, 1), line:line + 1, :] = value[None]

                each = [marks_ref[2 * source + side, 2 * column + (1 - side if kind else side)] for kind in kinds]
                slot_dots(rows_held.at[n % 2, pl.ds(0, len(rows))], held.at[n % 2], each, exp_dev, put)

    return pl.pallas_call(
        body,
        in_specs=[ANYWHERE] * (len(blocks) + len(flat)) + [LOCAL] * 2,
        out_specs=LOCAL,
        out_shape=jax.ShapeDtypeStruct(message.shape, F32),
        input_output_aliases={1 + len(blocks) + len(flat): 0},
        scratch_shapes=[
            pltpu.VMEM((2, tok, width), BF16),
            pltpu.VMEM((2, most, count, width), BF16),
            pltpu.SemaphoreType.DMA((2,)),
            pltpu.SemaphoreType.DMA((2, most)),
        ],
        cost_estimate=pl.CostEstimate(
            flops=2 * len(flat) * tok * count * width, bytes_accessed=4 * len(flat) * count * width, transcendentals=0
        ),
        name="meet",
    )(*blocks, *flat, marks, message)


def last_dots(block, rows, marks, exp_dev):
    tok, length = block.shape[0], marks.shape[0] // 2

    def body(block_ref, rows_ref, marks_ref, out_ref):
        side, place, _ = spot(length)

        def put(kind, e, value):
            out_ref[e:e + 1, :] = value

        mark = marks_ref[2 * place + side, 2 * place + 1 - side]
        slot_dots(rows_ref, block_ref, [mark], exp_dev, put)

    return pl.pallas_call(
        body,
        in_specs=[LOCAL] * 3,
        out_specs=LOCAL,
        out_shape=jax.ShapeDtypeStruct((exp_dev, tok), F32),
        cost_estimate=pl.CostEstimate(
            flops=2 * tok * rows.size, bytes_accessed=2 * (block.size + rows.size), transcendentals=0
        ),
        name="last_dots",
    )(block, rows[None], marks)


def finish(got, late, mix, probability, counts, scale, prob_sums, tokens, dp, exp_dev, share):
    experts, tok = mix.shape
    length, width = got.shape[0], tokens.shape[1]
    ep, piece = 2 * length, width // dp
    far = got.shape[1] // (2 * exp_dev) - 1
    lanes = -(-(piece + experts) // 128) * 128

    def body(scale_ref, got_ref, late_ref, mix_ref, prob_ref, counts_ref, sums_ref, tokens_ref, grad_ref, sent_ref, dots_ref):
        side, place, _ = spot(length)
        square = (experts, experts)
        same = lax.broadcasted_iota(jnp.int32, square, 0) == lax.broadcasted_iota(jnp.int32, square, 1)
        total = jnp.sum(counts_ref[...], axis=0, keepdims=True) * share
        push = scale_ref[0] * experts * jnp.sum(jnp.where(same, total, 0.0), axis=1, keepdims=True)
        probability = prob_ref[...]
        spread = probability * (push - jnp.sum(probability * push, axis=0, keepdims=True))
        for c in range(length):
            for kind in range(2):
                value = got_ref[c, kind * exp_dev:(kind + 1) * exp_dev, :]
                for i in range(1, far + 1):
                    line = (2 * i + kind) * exp_dev
                    if c - i >= 0:
                        value += jnp.where(c - i > place, got_ref[c - i, line:line + exp_dev, :], 0.0)
                    if c + i < length:
                        value += jnp.where(c + i < place, got_ref[c + i, line:line + exp_dev, :], 0.0)
                if kind:
                    value += jnp.where(c == place, late_ref[...], 0.0)
                at = 2 * c + jnp.where(side == kind, 0, 1)
                dots_ref[pl.ds(at, 1), :, :] = value[None]
        dots = jnp.concatenate([dots_ref[j] for j in range(ep)], axis=0)
        mixed = mix_ref[...] * dots
        grad = (spread + (mixed - mix_ref[...] * jnp.sum(mixed, axis=0, keepdims=True))).astype(BF16)
        grad_ref[...] = grad
        term = jnp.dot(grad, tokens_ref[...], preferred_element_type=F32)
        for d in range(dp):
            part = term[:, d * piece:(d + 1) * piece]
            for j in range(ep):
                sent_ref[j * dp + d, :, :piece] = part[j * exp_dev:(j + 1) * exp_dev]
        sums = jnp.broadcast_to(sums_ref[...][None], (ep * dp, exp_dev, experts))
        sent_ref[:, :, piece:piece + experts] = sums
        if lanes > piece + experts:
            sent_ref[:, :, piece + experts:] = jnp.zeros((ep * dp, exp_dev, lanes - piece - experts), F32)

    return pl.pallas_call(
        body,
        in_specs=[SCALARS] + [LOCAL] * 7,
        out_specs=[LOCAL] * 2,
        out_shape=[
            jax.ShapeDtypeStruct((experts, tok), BF16),
            jax.ShapeDtypeStruct((ep * dp, exp_dev, lanes), F32),
        ],
        scratch_shapes=[pltpu.VMEM((ep, exp_dev, tok), F32)],
        cost_estimate=pl.CostEstimate(
            flops=2 * experts * tok * width, bytes_accessed=2 * tok * width + 4 * experts * width, transcendentals=0
        ),
        name="finish",
    )(scale, got, late, mix, probability, counts, prob_sums, tokens)


def on_device(tokens, out_grad, indices, expert_rows, router_weight, router_bias, balance_scale):
    tok, width = tokens.shape
    experts = router_weight.shape[1]
    exp_dev, capacity = expert_rows.shape[1], expert_rows.shape[3]
    ep, dp = lax.axis_size("ep"), lax.axis_size("dp")
    token_total = tok * ep * dp
    length = ep // 2
    reach = length // 2
    far = length - 1 - reach

    entries = exp_dev * capacity
    table = expert_rows.transpose(0, 1, 3, 2, 4).reshape(entries * ep, width)
    cross = [(j, j ^ 1) for j in range(ep)]
    leaving = list(split_rows(table, [(0, True)], ep))
    block, table, leaving[0] = lax.optimization_barrier((out_grad, table, leaving[0]))
    rest = list(split_rows(table, [(n, True) for n in range(1, length)] + [(n, False) for n in range(length)], ep))
    leaving, own = leaving + rest[:length - 1], rest[length - 1:]
    other = []
    for rows in leaving:
        other.append(lax.ppermute(rows, "ep", cross))

    def shift(x, *moves):
        pairs = [(z, to) for valid, by in moves for z in range(length) for to in [z + by] if valid(z) and 0 <= to < length]
        return lax.ppermute(x, "ep", [(2 * z + s, 2 * to + s) for z, to in pairs for s in range(2)])

    below, above = [block], [block]
    for hop in range(reach):
        below.append(shift(below[-1], (lambda z: z >= hop, 1)))
        above.append(shift(above[-1], (lambda z: z + hop < length, -1)))
    blocks = below[:0:-1] + [block] + above[1:]

    guests = []
    for i in range(1, far + 1):
        d = reach + i
        moves = ((lambda z: z + d < length, i), (lambda z: z - d >= 0, -i))
        guests.append([])
        for rows in (own, other):
            guests[-1].append(shift(rows[length - 1 - d], *moves))

    chosen, _ = lax.optimization_barrier((indices.T, rest[0]))
    mine = slot_marks(chosen, ep, exp_dev)
    marks = lax.all_to_all(mine, "ep", split_axis=0, concat_axis=0, tiled=True)
    counts = jnp.sum((marks >= 0).astype(F32), axis=(0, 3)).reshape(1, experts)
    counts = lax.all_to_all(jnp.broadcast_to(counts, (dp, experts)), "dp", split_axis=0, concat_axis=0, tiled=True)

    tokens, _ = lax.optimization_barrier((tokens, rest[0]))
    probability, mix, prob_sums = router(router_weight.T, tokens, router_bias[:, None], mine[0])

    def job(n, kinds, hops):
        def plan():
            _, place, _ = spot(length)
            source = source_at(length, n)
            return source, place, source - place + hops

        return [(own, other)[kind][n] for kind in kinds], kinds, plan, 0

    def guest_job(i):
        def plan():
            _, place, low = spot(length)
            column = place + jnp.where(low, -i, i)
            source = place + jnp.where(low, reach, -reach)
            there = (column >= 0) & (column < length) & (source >= 0) & (source < length)
            which = jnp.where(there, jnp.where(low, 1, 0), -1)
            return jnp.clip(source, 0, length - 1), jnp.clip(column, 0, length - 1), which

        return guests[i - 1], (0, 1), plan, 2 * i * exp_dev

    message = jnp.zeros((length, 2 * exp_dev * (1 + far), tok), F32)
    near = {0: (0, 1), length - 2: (0,), length - 1: (0,)}
    calls = [(blocks[reach - 1:reach + 2], [job(n, kinds, 1) for n, kinds in near.items()])]
    middle = [job(n, (0, 1), reach) for n in range(1, length - 2)]
    calls.append((blocks, middle + [job(length - 2, (1,), reach)]))
    if far:
        calls.append((blocks[::2 * reach], [guest_job(i) for i in range(1, far + 1)]))
    for near_by, jobs in calls:
        message = meet(near_by, jobs, marks, message, exp_dev)
    rows_of = [[2 * z + s for z in range(length)] for s in range(2)]
    got = lax.all_to_all(message, "ep", split_axis=0, concat_axis=0, tiled=True, axis_index_groups=rows_of)
    late = last_dots(out_grad, other[length - 1], marks, exp_dev)

    share = 1.0 / (token_total * indices.shape[1])
    logit_grad, sent = finish(
        got, late, mix, probability, counts, balance_scale, prob_sums, tokens, dp, exp_dev, share
    )
    token_grad = lax.dot_general(
        logit_grad, router_weight, (((0,), (1,)), ((), ())), preferred_element_type=F32
    ).astype(BF16)
    summed = jnp.sum(lax.all_to_all(sent, ("ep", "dp"), split_axis=0, concat_axis=0, tiled=True), axis=0)
    share_of = jnp.sum(counts, axis=0) * share
    piece = width // dp
    weight_grad = summed[:, :piece].T / math.sqrt(token_total)
    balance_loss = (experts * jnp.sum(share_of * (summed[0, piece:piece + experts] / token_total))).reshape(1)
    return (token_grad, weight_grad, balance_loss)


def solution(mesh):
    placed = (
        P(("ep", "dp"), None),
        P(("ep", "dp"), None),
        P(("ep", "dp"), None),
        P("dp", "ep", None, None, None),
        P(),
        P(),
        P(),
    )

    return jax.shard_map(
        on_device,
        mesh=mesh,
        in_specs=placed,
        out_specs=(P(("ep", "dp"), None), P("dp", "ep"), P()),
        check_vma=False,
    )
```

profile of v0, /device:TPU:0, one launch (start us, length us, event | category | flops | bytes accessed | tf_op | source)
XLA Modules:
  0.0 145.9 jit_solution(6550724002367556695)
XLA Ops:
  0.6 5.2 %split_rows.2 = bf16[144,2880]{1,0:T(8,128)(2,1)} custom-call(bf16[1152,2880]{1,0:T(8,128)(2,1)} %bitcast.21), custom_call_target="tpu_custom_call" | custom-call | flops 106168320 | bytes 9953280 | tf_op jit(solution)/shard_map/split_rows/pallas_call | solution.py:57
  5.9 5.0 %collective-permute-start = (bf16[192,2880]{1,0:T(8,128)(2,1)S(1)}, bf16[192,2880]{1,0:T(8,128)(2,1)S(1)}, u32[]{:S(2)}, u32[]{:S(2)}) collective-permute-start(bf16[192,2880]{1,0:T(8,128)(2,1)S(1)} %copy-done), channel_id=1, source_target_pairs={{0,8},{4,12},{8,16},{12,20},{16,24},{20,28},{1,9},{5,13},{9,17},{1... | collective-permute-start | bytes 3317768 | tf_op jit(solution)/shard_map/ppermute | solution.py:319
  13.8 7.3 %split_rows.3 = (bf16[144,2880]{1,0:T(8,128)(2,1)}, bf16[144,2880]{1,0:T(8,128)(2,1)}, bf16[144,2880]{1,0:T(8,128)(2,1)}, bf16[144,2880]{1,0:T(8,128)(2,1)}, bf1...) custom-call(bf16[1152,2880]{1,0:T(8,128)(2,1)} %bitcast.22), custom_call_target="tpu_custom_call" | custom-call | flops 743178240 | bytes 9953280 | tf_op jit(solution)/shard_map/split_rows/pallas_call | solution.py:57
  23.1 11.8 %collective-permute-done.refs_0_.refs_1_ = bf16[192,2880]{1,0:T(8,128)(2,1)S(1)} collective-permute-done((bf16[192,2880]{1,0:T(8,128)(2,1)S(1)}, bf16[192,2880]{1,0:T(8,128)(2,1)S(1)}, u32[]{:S(2)}, u32[]{:S(2)}) %collective-permute-start) | collective-permute-done | bytes 1105952 | tf_op jit(solution)/shard_map/ppermute | solution.py:319
  35.0 1.7 %collective-permute-start.1 = (bf16[192,2880]{1,0:T(8,128)(2,1)S(1)}, bf16[192,2880]{1,0:T(8,128)(2,1)}, u32[]{:S(2)}, u32[]{:S(2)}) collective-permute-start(bf16[192,2880]{1,0:T(8,128)(2,1)S(1)} %collective-permute-done.refs_0_.refs_1_), channel_id=1, source_target_pairs={{8,16},{12,20},{16,24},{20,28},{9,17},{13,21},{17,25},{21,29},{10,... | collective-permute-start | bytes 3317768 | tf_op jit(solution)/shard_map/ppermute | solution.py:319
  36.7 2.5 %collective-permute-done.2.refs_2_.refs_3_ = bf16[192,2880]{1,0:T(8,128)(2,1)S(1)} collective-permute-done((bf16[192,2880]{1,0:T(8,128)(2,1)S(1)}, bf16[192,2880]{1,0:T(8,128)(2,1)S(1)}, u32[]{:S(2)}, u32[]{:S(2)}) %collective-permute-start.2) | collective-permute-done | bytes 1105952 | tf_op jit(solution)/shard_map/ppermute | solution.py:319
  40.5 6.2 %collective-permute-start.4 = (bf16[144,2880]{1,0:T(8,128)(2,1)}, bf16[144,2880]{1,0:T(8,128)(2,1)}, u32[]{:S(2)}, u32[]{:S(2)}) collective-permute-start(bf16[144,2880]{1,0:T(8,128)(2,1)} %get-tuple-element.22.refs_3_), channel_id=1, source_target_pairs={{0,8},{4,12},{24,16},{28,20},{1,9},{5,13},{25,17},{29,21},{2,10},{... | collective-permute-start | bytes 2488328 | tf_op jit(solution)/shard_map/ppermute | solution.py:319
  46.7 5.8 %collective-permute-done.7.refs_6_ = bf16[144,2880]{1,0:T(8,128)(2,1)} collective-permute-done((bf16[144,2880]{1,0:T(8,128)(2,1)}, bf16[144,2880]{1,0:T(8,128)(2,1)}, u32[]{:S(2)}, u32[]{:S(2)}) %collective-permute-start.7) | collective-permute-done | bytes 829472 | tf_op jit(solution)/shard_map/ppermute | solution.py:315
  52.5 5.6 %collective-permute-start.6 = (bf16[144,2880]{1,0:T(8,128)(2,1)}, bf16[144,2880]{1,0:T(8,128)(2,1)}, u32[]{:S(2)}, u32[]{:S(2)}) collective-permute-start(bf16[144,2880]{1,0:T(8,128)(2,1)} %collective-permute-done.5.refs_4_), channel_id=1, source_target_pairs={{0,8},{4,12},{24,16},{28,20},{1,9},{5,13},{25,17},{29,21},{2,10},{... | collective-permute-start | bytes 2488328 | tf_op jit(solution)/shard_map/ppermute | solution.py:319
  59.6 4.6 %all-to-all-start = ((s32[8,8,4,192]{3,2,1,0:T(4,128)}), s32[8,8,4,192]{3,2,1,0:T(4,128)S(1)}, u32[]{:S(2)}, u32[]{:S(2)}) async-start(s32[8,8,4,192]{3,2,1,0:T(4,128)} %slot_marks.1), calls=%async_computation | async-start | bytes 524288 | tf_op jit(solution)/shard_map/all_to_all | solution.py:337
  64.2 6.0 %collective-permute-done.8.refs_7_ = bf16[144,2880]{1,0:T(8,128)(2,1)} collective-permute-done((bf16[144,2880]{1,0:T(8,128)(2,1)}, bf16[144,2880]{1,0:T(8,128)(2,1)}, u32[]{:S(2)}, u32[]{:S(2)}) %collective-permute-start.8) | collective-permute-done | bytes 829472 | tf_op jit(solution)/shard_map/ppermute | solution.py:315
  70.3 1.9 %collective-permute-start.9 = (bf16[144,2880]{1,0:T(8,128)(2,1)}, bf16[144,2880]{1,0:T(8,128)(2,1)S(1)}, u32[]{:S(2)}, u32[]{:S(2)}) collective-permute-start(bf16[144,2880]{1,0:T(8,128)(2,1)} %get-tuple-element.30), channel_id=1, source_target_pairs={{0,4},{4,0},{8,12},{12,8},{16,20},{20,16},{24,28},{28,24},{1,5},{5... | collective-permute-start | bytes 2488328 | tf_op jit(solution)/shard_map/ppermute | solution.py:315
  72.2 18.1 %all-to-all-done.refs_7_.refs_8_.refs_4_.marks_ref = s32[8,8,4,192]{3,2,1,0:T(4,128)S(1)} async-done(((s32[8,8,4,192]{3,2,1,0:T(4,128)}), s32[8,8,4,192]{3,2,1,0:T(4,128)S(1)}, u32[]{:S(2)}, u32[]{:S(2)}) %all-to-all-start) | async-done | bytes 196640 | tf_op jit(solution)/shard_map/all_to_all | solution.py:337
  91.1 3.2 %all-to-all-start.2 = ((f32[4,1,32]{2,1,0:T(1,128)}), f32[4,1,32]{2,1,0:T(1,128)S(1)}, u32[]{:S(2)}, u32[]{:S(2)}) async-start(f32[4,1,32]{2,1,0:T(1,128)} %broadcast_in_dim.20), calls=%async_computation.2 | async-start | bytes 4096 | tf_op jit(solution)/shard_map/all_to_all | solution.py:339
  95.0 4.3 %meet.3.refs_9_ = f32[4,16,192]{2,1,0:T(8,128)} custom-call(bf16[192,2880]{1,0:T(8,128)(2,1)} %copy-done.2, bf16[192,2880]{1,0:T(8,128)(2,1)} %block_ref.1, bf16[192,2880]{1,0:T(8,128)(2,1)} %copy-done.3, bf16[144,2880]{1,0:T(8,128)(2,1)} %get-tuple-element.22.refs_3_, ...), custom_call_target="tpu_custom_call", output_to_operand_aliasing={{}: (8, {})} | custom-call | flops 637009920 | bytes 6635520 | tf_op jit(solution)/shard_map/meet/pallas_call | solution.py:195
  99.3 4.6 %meet.4.refs_5_ = f32[4,16,192]{2,1,0:T(8,128)} custom-call(bf16[192,2880]{1,0:T(8,128)(2,1)} %collective-permute-done.1.refs_0_, bf16[192,2880]{1,0:T(8,128)(2,1)} %copy-done.2, bf16[192,2880]{1,0:T(8,128)(2,1)} %block_ref.1, bf16[192,2880]{1,0:T(8,128)(2,1)} %copy-done.3, ...), custom_call_target="tpu_custom_call", output_to_operand_aliasing={{}: (9, {})} | custom-call | flops 477757440 | bytes 4976640 | tf_op jit(solution)/shard_map/meet/pallas_call | solution.py:195
  103.9 1.7 %meet.5 = f32[4,16,192]{2,1,0:T(8,128)} custom-call(bf16[192,2880]{1,0:T(8,128)(2,1)} %collective-permute-done.1.refs_0_, bf16[192,2880]{1,0:T(8,128)(2,1)} %collective-permute-done.3.refs_4_.refs_1_, bf16[144,2880]{1,0:T(8,128)(2,1)} %collective-permute-done.4.refs_2_, ...), custom_call_target="tpu_custom_call", output_to_operand_aliasing={{}: (5, {})} | custom-call | flops 318504960 | bytes 3317760 | tf_op jit(solution)/shard_map/meet/pallas_call | solution.py:195
  105.6 6.1 %all-to-all-start.1 = ((f32[4,16,192]{2,1,0:T(8,128)}), f32[4,16,192]{2,1,0:T(8,128)S(1)}, u32[]{:S(2)}, u32[]{:S(2)}) async-start(f32[4,16,192]{2,1,0:T(8,128)} %meet.5), calls=%async_computation.1 | async-start | bytes 131072 | tf_op jit(solution)/shard_map/all_to_all | solution.py:373
  114.4 2.4 %router.1 = (f32[32,192]{1,0:T(8,128)}, f32[32,192]{1,0:T(8,128)}, f32[1,32]{1,0:T(1,128)}) custom-call(bf16[32,2880]{1,0:T(8,128)(2,1)} %bitcast.24, bf16[192,2880]{1,0:T(8,128)(2,1)} %tokens_ref.1, f32[32,1]{1,0:T(8,128)} %copy.15.bias_ref, s32[8,4,192]{2,1,0:T(4,128)} %slice_bitcast_fusion.marks_ref), custom_call_target="tpu_custom_call" | custom-call | flops 35389440 | bytes 1290240 | tf_op jit(solution)/shard_map/router/pallas_call | solution.py:115
  117.7 2.7 %last_dots.1.late_ref = f32[4,192]{1,0:T(4,128)} custom-call(bf16[192,2880]{1,0:T(8,128)(2,1)} %block_ref.1, bf16[1,144,2880]{2,1,0:T(8,128)(2,1)} %bitcast.23, s32[8,8,4,192]{3,2,1,0:T(4,128)} %copy-done.1), custom_call_target="tpu_custom_call" | custom-call | flops 159252480 | bytes 1935360 | tf_op jit(solution)/shard_map/last_dots/pallas_call | solution.py:226
  121.0 2.6 %finish.1 = (bf16[32,192]{1,0:T(8,128)(2,1)}, f32[32,4,768]{2,1,0:T(4,128)}) custom-call(f32[1]{0:T(128)S(6)} %copy.19.scale_ref, f32[4,16,192]{2,1,0:T(8,128)} %copy-done.6, f32[4,192]{1,0:T(4,128)} %last_dots.1.late_ref, f32[32,192]{1,0:T(8,128)} %get-tuple-element.32.mix_ref, f32[32,192]{1,0:T(8,128)} %get-tuple-element.33.prob_ref, f32[4,32]{1,0:T(4,128)} %bitcast.25, ...), custom_call_target="tpu_custom_call" | custom-call | flops 35389440 | bytes 1474560 | tf_op jit(solution)/shard_map/finish/pallas_call | solution.py:280
  123.6 5.9 %all-to-all-start.3 = ((f32[32,4,768]{2,1,0:T(4,128)}), f32[32,4,768]{2,1,0:T(4,128)S(1)}, u32[]{:S(2)}, u32[]{:S(2)}) async-start(f32[32,4,768]{2,1,0:T(4,128)} %get-tuple-element.36), calls=%async_computation.3 | async-start | bytes 786432 | tf_op jit(solution)/shard_map/all_to_all | solution.py:383
  129.5 2.2 %convolution_convert_fusion = bf16[192,2880]{1,0:T(8,128)(2,1)} fusion(bf16[32,192]{1,0:T(8,128)(2,1)} %get-tuple-element.35, bf16[2880,32]{0,1:T(8,128)(2,1)S(1)} %copy-done.5), kind=kOutput, calls=%fused_computation | convolution fusion | flops 35942400 | bytes 1302528 | tf_op jit(solution)/shard_map/dot_general | solution.py:380
  131.7 11.0 %all-to-all-done.3 = f32[32,4,768]{2,1,0:T(4,128)S(1)} async-done(((f32[32,4,768]{2,1,0:T(4,128)}), f32[32,4,768]{2,1,0:T(4,128)S(1)}, u32[]{:S(2)}, u32[]{:S(2)}) %all-to-all-start.3) | async-done | bytes 393248 | tf_op jit(solution)/shard_map/all_to_all | solution.py:383
  (44 shorter events, 14.2 us)
Async XLA Ops:
  0.6 5.2 %copy-start = (bf16[192,2880]{1,0:T(8,128)(2,1)S(1)}, bf16[192,2880]{1,0:T(8,128)(2,1)}, u32[]{:S(2)}) copy-start(bf16[192,2880]{1,0:T(8,128)(2,1)} %block_ref.1) | copy-start | bytes 3317764
  5.9 29.1 %collective-permute-start = (bf16[192,2880]{1,0:T(8,128)(2,1)S(1)}, bf16[192,2880]{1,0:T(8,128)(2,1)S(1)}, u32[]{:S(2)}, u32[]{:S(2)}) collective-permute-start(bf16[192,2880]{1,0:T(8,128)(2,1)S(1)} %copy-done), channel_id=1, source_target_pairs={{0,8},{4,12},{8,16},{12,20},{16,24},{20,28},{1,9},{5,13},{9,17},{1... | collective-permute-start | bytes 3317768 | tf_op jit(solution)/shard_map/ppermute | solution.py:319
  10.9 28.3 %collective-permute-start.2 = (bf16[192,2880]{1,0:T(8,128)(2,1)S(1)}, bf16[192,2880]{1,0:T(8,128)(2,1)S(1)}, u32[]{:S(2)}, u32[]{:S(2)}) collective-permute-start(bf16[192,2880]{1,0:T(8,128)(2,1)S(1)} %copy-done), channel_id=1, source_target_pairs={{8,0},{12,4},{16,8},{20,12},{24,16},{28,20},{9,1},{13,5},{17,9},{2... | collective-permute-start | bytes 3317768 | tf_op jit(solution)/shard_map/ppermute | solution.py:319
  12.2 28.3 %collective-permute-start.5 = (bf16[144,2880]{1,0:T(8,128)(2,1)}, bf16[144,2880]{1,0:T(8,128)(2,1)}, u32[]{:S(2)}, u32[]{:S(2)}) collective-permute-start(bf16[144,2880]{1,0:T(8,128)(2,1)} %split_rows.2), channel_id=1, source_target_pairs={{0,4},{4,0},{8,12},{12,8},{16,20},{20,16},{24,28},{28,24},{1,5},{5... | collective-permute-start | bytes 2488328 | tf_op jit(solution)/shard_map/ppermute | solution.py:315
  21.1 31.4 %collective-permute-start.7 = (bf16[144,2880]{1,0:T(8,128)(2,1)}, bf16[144,2880]{1,0:T(8,128)(2,1)}, u32[]{:S(2)}, u32[]{:S(2)}) collective-permute-start(bf16[144,2880]{1,0:T(8,128)(2,1)} %get-tuple-element.24), channel_id=1, source_target_pairs={{0,4},{4,0},{8,12},{12,8},{16,20},{20,16},{24,28},{28,24},{1,5},{5... | collective-permute-start | bytes 2488328 | tf_op jit(solution)/shard_map/ppermute | solution.py:315
  21.6 48.7 %collective-permute-start.8 = (bf16[144,2880]{1,0:T(8,128)(2,1)}, bf16[144,2880]{1,0:T(8,128)(2,1)}, u32[]{:S(2)}, u32[]{:S(2)}) collective-permute-start(bf16[144,2880]{1,0:T(8,128)(2,1)} %get-tuple-element.27), channel_id=1, source_target_pairs={{0,4},{4,0},{8,12},{12,8},{16,20},{20,16},{24,28},{28,24},{1,5},{5... | collective-permute-start | bytes 2488328 | tf_op jit(solution)/shard_map/ppermute | solution.py:315
  35.0 60.0 %copy-start.2 = (bf16[192,2880]{1,0:T(8,128)(2,1)}, bf16[192,2880]{1,0:T(8,128)(2,1)S(1)}, u32[]{:S(2)}) copy-start(bf16[192,2880]{1,0:T(8,128)(2,1)S(1)} %collective-permute-done.refs_0_.refs_1_) | copy-start | bytes 3317764
  35.0 64.3 %collective-permute-start.1 = (bf16[192,2880]{1,0:T(8,128)(2,1)S(1)}, bf16[192,2880]{1,0:T(8,128)(2,1)}, u32[]{:S(2)}, u32[]{:S(2)}) collective-permute-start(bf16[192,2880]{1,0:T(8,128)(2,1)S(1)} %collective-permute-done.refs_0_.refs_1_), channel_id=1, source_target_pairs={{8,16},{12,20},{16,24},{20,28},{9,17},{13,21},{17,25},{21,29},{10,... | collective-permute-start | bytes 3317768 | tf_op jit(solution)/shard_map/ppermute | solution.py:319
  39.2 55.8 %copy-start.3 = (bf16[192,2880]{1,0:T(8,128)(2,1)}, bf16[192,2880]{1,0:T(8,128)(2,1)S(1)}, u32[]{:S(2)}) copy-start(bf16[192,2880]{1,0:T(8,128)(2,1)S(1)} %collective-permute-done.2.refs_2_.refs_3_) | copy-start | bytes 3317764
  39.2 60.1 %collective-permute-start.3 = (bf16[192,2880]{1,0:T(8,128)(2,1)S(1)}, bf16[192,2880]{1,0:T(8,128)(2,1)}, u32[]{:S(2)}, u32[]{:S(2)}) collective-permute-start(bf16[192,2880]{1,0:T(8,128)(2,1)S(1)} %collective-permute-done.2.refs_2_.refs_3_), channel_id=1, source_target_pairs={{8,0},{12,4},{16,8},{20,12},{9,1},{13,5},{17,9},{21,13},{10,2},{14... | collective-permute-start | bytes 3317768 | tf_op jit(solution)/shard_map/ppermute | solution.py:319
  40.5 63.4 %collective-permute-start.4 = (bf16[144,2880]{1,0:T(8,128)(2,1)}, bf16[144,2880]{1,0:T(8,128)(2,1)}, u32[]{:S(2)}, u32[]{:S(2)}) collective-permute-start(bf16[144,2880]{1,0:T(8,128)(2,1)} %get-tuple-element.22.refs_3_), channel_id=1, source_target_pairs={{0,8},{4,12},{24,16},{28,20},{1,9},{5,13},{25,17},{29,21},{2,10},{... | collective-permute-start | bytes 2488328 | tf_op jit(solution)/shard_map/ppermute | solution.py:319
  52.5 51.4 %collective-permute-start.6 = (bf16[144,2880]{1,0:T(8,128)(2,1)}, bf16[144,2880]{1,0:T(8,128)(2,1)}, u32[]{:S(2)}, u32[]{:S(2)}) collective-permute-start(bf16[144,2880]{1,0:T(8,128)(2,1)} %collective-permute-done.5.refs_4_), channel_id=1, source_target_pairs={{0,8},{4,12},{24,16},{28,20},{1,9},{5,13},{25,17},{29,21},{2,10},{... | collective-permute-start | bytes 2488328 | tf_op jit(solution)/shard_map/ppermute | solution.py:319
  59.6 30.6 %all-to-all-start = ((s32[8,8,4,192]{3,2,1,0:T(4,128)}), s32[8,8,4,192]{3,2,1,0:T(4,128)S(1)}, u32[]{:S(2)}, u32[]{:S(2)}) async-start(s32[8,8,4,192]{3,2,1,0:T(4,128)} %slot_marks.1), calls=%async_computation | async-start | bytes 524288 | tf_op jit(solution)/shard_map/all_to_all | solution.py:337
  70.3 46.5 %collective-permute-start.9 = (bf16[144,2880]{1,0:T(8,128)(2,1)}, bf16[144,2880]{1,0:T(8,128)(2,1)S(1)}, u32[]{:S(2)}, u32[]{:S(2)}) collective-permute-start(bf16[144,2880]{1,0:T(8,128)(2,1)} %get-tuple-element.30), channel_id=1, source_target_pairs={{0,4},{4,0},{8,12},{12,8},{16,20},{20,16},{24,28},{28,24},{1,5},{5... | collective-permute-start | bytes 2488328 | tf_op jit(solution)/shard_map/ppermute | solution.py:315
  90.2 4.7 %copy-start.1 = (s32[8,8,4,192]{3,2,1,0:T(4,128)}, s32[8,8,4,192]{3,2,1,0:T(4,128)S(1)}, u32[]{:S(2)}) copy-start(s32[8,8,4,192]{3,2,1,0:T(4,128)S(1)} %all-to-all-done.refs_7_.refs_8_.refs_4_.marks_ref) | copy-start | bytes 589828
  91.1 14.5 %all-to-all-start.2 = ((f32[4,1,32]{2,1,0:T(1,128)}), f32[4,1,32]{2,1,0:T(1,128)S(1)}, u32[]{:S(2)}, u32[]{:S(2)}) async-start(f32[4,1,32]{2,1,0:T(1,128)} %broadcast_in_dim.20), calls=%async_computation.2 | async-start | bytes 4096 | tf_op jit(solution)/shard_map/all_to_all | solution.py:339
  103.9 9.2 %copy-start.9 = (f32[32]{0:T(128)S(1)}, f32[32]{0:T(128)}, u32[]{:S(2)}) copy-start(f32[32]{0:T(128)} %param.12) | copy-start | bytes 388
  105.6 14.7 %copy-start.7 = (f32[4,1,32]{2,1,0:T(1,128)}, f32[4,1,32]{2,1,0:T(1,128)S(1)}, u32[]{:S(2)}) copy-start(f32[4,1,32]{2,1,0:T(1,128)S(1)} %all-to-all-done.2) | copy-start | bytes 1540
  105.6 14.7 %all-to-all-start.1 = ((f32[4,16,192]{2,1,0:T(8,128)}), f32[4,16,192]{2,1,0:T(8,128)S(1)}, u32[]{:S(2)}, u32[]{:S(2)}) async-start(f32[4,16,192]{2,1,0:T(8,128)} %meet.5), calls=%async_computation.1 | async-start | bytes 131072 | tf_op jit(solution)/shard_map/all_to_all | solution.py:373
  116.8 0.9 copy-start.4
  120.3 9.2 %copy-start.5 = (bf16[2880,32]{0,1:T(8,128)(2,1)S(1)}, bf16[2880,32]{0,1:T(8,128)(2,1)}, u32[]{:S(2)}) copy-start(bf16[2880,32]{0,1:T(8,128)(2,1)} %param.11) | copy-start | bytes 552964
  120.4 0.6 copy-start.6
  120.4 9.1 %copy-start.8 = (f32[4,1,32]{2,1,0:T(1,128)S(1)}, f32[4,1,32]{2,1,0:T(1,128)}, u32[]{:S(2)}) copy-start(f32[4,1,32]{2,1,0:T(1,128)} %copy-done.7) | copy-start | bytes 1540
  123.6 19.1 %all-to-all-start.3 = ((f32[32,4,768]{2,1,0:T(4,128)}), f32[32,4,768]{2,1,0:T(4,128)S(1)}, u32[]{:S(2)}, u32[]{:S(2)}) async-start(f32[32,4,768]{2,1,0:T(4,128)} %get-tuple-element.36), calls=%async_computation.3 | async-start | bytes 786432 | tf_op jit(solution)/shard_map/all_to_all | solution.py:383
where the time goes:
time: 147 us; the launch traced here: 146 us
  waiting for transfers between devices  55.2 us (38%)
  starting transfers between devices  46.3 us (31%)
  Pallas kernels  32.4 us (22%)
  local copies, waits for them, and re-layouts  4.93 us (3%)
  between operations  3.25 us (2%)
  matrix products  2.2 us (1%)
  other arithmetic  1.54 us (1%)
    ppermute x6, starting transfers between devices, shift(): lax.ppermute(x, 'ep', [(2 * z + s, 2 * to + s) for z, to in pairs for s i...  21.1 us
    all_to_all x1, waiting for transfers between devices, on_device(): marks = lax.all_to_all(mine, 'ep', split_axis=0, concat_axis=0, tiled=True)  18.1 us
    ppermute x6, waiting for transfers between devices, shift(): lax.ppermute(x, 'ep', [(2 * z + s, 2 * to + s) for z, to in pairs for s i...  14.4 us
    pallas_call x2, Pallas kernels, split_rows(): pl.pallas_call(body, grid=(parts // group,), in_specs=[pl.BlockSpec((grou...  12.6 us
    ppermute x4, waiting for transfers between devices, on_device(): other.append(lax.ppermute(rows, 'ep', cross))  11.8 us
    all_to_all x1, waiting for transfers between devices, on_device(): lax.all_to_all(sent, ('ep', 'dp'), split_axis=0, concat_axis=0, tiled=True)  11 us
    pallas_call x3, Pallas kernels, meet(): pl.pallas_call(body, in_specs=[ANYWHERE] * (len(blocks) + len(flat)) + [L...  10.6 us
    all_to_all x1, starting transfers between devices, on_device(): lax.all_to_all(message, 'ep', split_axis=0, concat_axis=0, tiled=True, ax...  6.06 us
  transfers between devices with their start and end apart: 14, of which 6 were waited for; matrix products, arithmetic and copies ran while one was open for 4% of the time, Pallas kernels for 17%

commit v1 on v0

--- a/solution.py
+++ b/solution.py
@@ -141,7 +141,7 @@
 
 def meet(blocks, jobs, marks, message, exp_dev):
     tok, width = blocks[0].shape
-    length = message.shape[0]
+    length = marks.shape[0] // 2
     flat = [r for job in jobs for r in job[0]]
     count = flat[0].shape[0]
     most = max(len(job[0]) for job in jobs)
@@ -181,13 +181,13 @@
             def _(n=n):
                 pltpu.make_async_copy(block_refs[0], held.at[n % 2], block_sem.at[n % 2]).wait()
                 rows, kinds = jobs[n][:2]
-                source, column, _ = plans[n]
+                source, column, _, target = plans[n]
                 for k in range(len(rows)):
                     rows_copy(n, k).wait()
 
                 def put(k, e, value):
                     line = jobs[n][3] + kinds[k] * exp_dev + e
-                    out_ref[pl.ds(source, 1), line:line + 1, :] = value[None]
+                    out_ref[pl.ds(target, 1), line:line + 1, :] = value[None]
 
                 each = [marks_ref[2 * source + side, 2 * column + (1 - side if kind else side)] for kind in kinds]
                 slot_dots(rows_held.at[n % 2, pl.ds(0, len(rows))], held.at[n % 2], each, exp_dev, put)
@@ -235,14 +235,14 @@
     )(block, rows[None], marks)
 
 
-def finish(got, late, mix, probability, counts, scale, prob_sums, tokens, dp, exp_dev, share):
+def finish(got, guest, late, mix, probability, counts, scale, prob_sums, tokens, dp, exp_dev, share):
     experts, tok = mix.shape
     length, width = got.shape[0], tokens.shape[1]
     ep, piece = 2 * length, width // dp
-    far = got.shape[1] // (2 * exp_dev) - 1
+    reach, far = length // 2, guest.shape[1] // (2 * exp_dev)
     lanes = -(-(piece + experts) // 128) * 128
 
-    def body(scale_ref, got_ref, late_ref, mix_ref, prob_ref, counts_ref, sums_ref, tokens_ref, grad_ref, sent_ref, dots_ref):
+    def body(scale_ref, got_ref, guest_ref, late_ref, mix_ref, prob_ref, counts_ref, sums_ref, tokens_ref, grad_ref, sent_ref, dots_ref):
         side, place, _ = spot(length)
         square = (experts, experts)
         same = lax.broadcasted_iota(jnp.int32, square, 0) == lax.broadcasted_iota(jnp.int32, square, 1)
@@ -254,11 +254,9 @@
             for kind in range(2):
                 value = got_ref[c, kind * exp_dev:(kind + 1) * exp_dev, :]
                 for i in range(1, far + 1):
-                    line = (2 * i + kind) * exp_dev
-                    if c - i >= 0:
-                        value += jnp.where(c - i > place, got_ref[c - i, line:line + exp_dev, :], 0.0)
-                    if c + i < length:
-                        value += jnp.where(c + i < place, got_ref[c + i, line:line + exp_dev, :], 0.0)
+                    line = (2 * (i - 1) + kind) * exp_dev
+                    column = place + jnp.where(place < reach, reach + i, -reach - i)
+                    value += jnp.where(c == column, guest_ref[0, line:line + exp_dev, :], 0.0)
                 if kind:
                     value += jnp.where(c == place, late_ref[...], 0.0)
                 at = 2 * c + jnp.where(side == kind, 0, 1)
@@ -279,7 +277,7 @@
 
     return pl.pallas_call(
         body,
-        in_specs=[SCALARS] + [LOCAL] * 7,
+        in_specs=[SCALARS] + [LOCAL] * 8,
         out_specs=[LOCAL] * 2,
         out_shape=[
             jax.ShapeDtypeStruct((experts, tok), BF16),
@@ -290,7 +288,7 @@
             flops=2 * experts * tok * width, bytes_accessed=2 * tok * width + 4 * experts * width, transcendentals=0
         ),
         name="finish",
-    )(scale, got, late, mix, probability, counts, prob_sums, tokens)
+    )(scale, got, guest, late, mix, probability, counts, prob_sums, tokens)
 
 
 def on_device(tokens, out_grad, indices, expert_rows, router_weight, router_bias, balance_scale):
@@ -299,6 +297,7 @@
     exp_dev, capacity = expert_rows.shape[1], expert_rows.shape[3]
     ep, dp = lax.axis_size("ep"), lax.axis_size("dp")
     token_total = tok * ep * dp
+    assert ep % 4 == 0
     length = ep // 2
     reach = length // 2
     far = length - 1 - reach
@@ -307,7 +306,8 @@
     table = expert_rows.transpose(0, 1, 3, 2, 4).reshape(entries * ep, width)
     cross = [(j, j ^ 1) for j in range(ep)]
     leaving = list(split_rows(table, [(0, True)], ep))
-    block, table, leaving[0] = lax.optimization_barrier((out_grad, table, leaving[0]))
+    table, leaving[0] = lax.optimization_barrier((table, leaving[0]))
+    block = out_grad
     rest = list(split_rows(table, [(n, True) for n in range(1, length)] + [(n, False) for n in range(length)], ep))
     leaving, own = leaving + rest[:length - 1], rest[length - 1:]
     other = []
@@ -345,37 +345,37 @@
         def plan():
             _, place, _ = spot(length)
             source = source_at(length, n)
-            return source, place, source - place + hops
+            return source, place, source - place + hops, source
 
         return [(own, other)[kind][n] for kind in kinds], kinds, plan, 0
 
-    def guest_job(i):
+    def guest_job(i, kind):
         def plan():
             _, place, low = spot(length)
             column = place + jnp.where(low, -i, i)
             source = place + jnp.where(low, reach, -reach)
-            there = (column >= 0) & (column < length) & (source >= 0) & (source < length)
+            there = (column >= 0) & (column < length)
             which = jnp.where(there, jnp.where(low, 1, 0), -1)
-            return jnp.clip(source, 0, length - 1), jnp.clip(column, 0, length - 1), which
-
-        return guests[i - 1], (0, 1), plan, 2 * i * exp_dev
-
-    message = jnp.zeros((length, 2 * exp_dev * (1 + far), tok), F32)
-    near = {0: (0, 1), length - 2: (0,), length - 1: (0,)}
-    calls = [(blocks[reach - 1:reach + 2], [job(n, kinds, 1) for n, kinds in near.items()])]
-    middle = [job(n, (0, 1), reach) for n in range(1, length - 2)]
-    calls.append((blocks, middle + [job(length - 2, (1,), reach)]))
-    if far:
-        calls.append((blocks[::2 * reach], [guest_job(i) for i in range(1, far + 1)]))
-    for near_by, jobs in calls:
-        message = meet(near_by, jobs, marks, message, exp_dev)
+            return source, jnp.clip(column, 0, length - 1), which, 0
+
+        return [guests[i - 1][kind]], (kind,), plan, 2 * (i - 1) * exp_dev
+
+    message = jnp.zeros((length, 2 * exp_dev, tok), F32)
+    near = [job(0, (0, 1), 1), job(length - 2, (0,), 1), job(length - 1, (0,), 1)]
+    message = meet(blocks[reach - 1:reach + 2], near, marks, message, exp_dev)
+    message = meet(blocks, [job(n, (0, 1), reach) for n in range(1, length - 2)], marks, message, exp_dev)
+    message = meet(blocks[reach - 1:reach + 2], [job(length - 2, (1,), 1)], marks, message, exp_dev)
     rows_of = [[2 * z + s for z in range(length)] for s in range(2)]
     got = lax.all_to_all(message, "ep", split_axis=0, concat_axis=0, tiled=True, axis_index_groups=rows_of)
+    guest = jnp.zeros((1, 2 * exp_dev * far, tok), F32)
+    for kind in range(2):
+        guest = meet(blocks[::2 * reach], [guest_job(i, kind) for i in range(1, far + 1)], marks, guest, exp_dev)
+    guest = shift(guest, (lambda z: 0 < z < reach, reach), (lambda z: reach <= z < length - 1, -reach))
     late = last_dots(out_grad, other[length - 1], marks, exp_dev)
 
     share = 1.0 / (token_total * indices.shape[1])
     logit_grad, sent = finish(
-        got, late, mix, probability, counts, balance_scale, prob_sums, tokens, dp, exp_dev, share
+        got, guest, late, mix, probability, counts, balance_scale, prob_sums, tokens, dp, exp_dev, share
     )
     token_grad = lax.dot_general(
         logit_grad, router_weight, (((0,), (1,)), ((), ())), preferred_element_type=F32

time: 147 us -> 178 us (1.21)
  waiting for transfers between devices: 55.2 us -> 76.7 us
  starting transfers between devices: 46.3 us -> 50.9 us
  Pallas kernels: 32.4 us -> 36.8 us
    ppermute x6 -> x7, waiting for transfers between devices: 14.4 us -> 28.3 us  [shift(): lax.ppermute(x, 'ep', [(2 * z + s, 2 * to + s) for z, to in pairs for s i...]
    ppermute x4, waiting for transfers between devices: 11.8 us -> 19.8 us  [on_device(): other.append(lax.ppermute(rows, 'ep', cross))]
    ppermute x6 -> x7, starting transfers between devices: 21.1 us -> 26.6 us  [shift(): lax.ppermute(x, 'ep', [(2 * z + s, 2 * to + s) for z, to in pairs for s i...]
    pallas_call x3 -> x5, Pallas kernels: 10.6 us -> 15 us  [meet(): pl.pallas_call(body, in_specs=[ANYWHERE] * (len(blocks) + len(flat)) + [L...]
    all_to_all x1, starting transfers between devices: 6.06 us -> 8 us  [on_device(): lax.all_to_all(message, 'ep', split_axis=0, concat_axis=0, tiled=True, ax...]
  transfers between devices with their start and end apart: 14 -> 15, of which waited for: 6 -> 6; matrix products, arithmetic and copies ran while one was open for 4% -> 4% of each run, Pallas kernels for 17% -> 19%
where the time goes in v1:
time: 178 us; the launch traced here: 177 us
  waiting for transfers between devices  76.7 us (43%)
  starting transfers between devices  50.9 us (29%)
  Pallas kernels  36.8 us (21%)
  local copies, waits for them, and re-layouts  5.46 us (3%)
  between operations  3.26 us (2%)
  matrix products  2.2 us (1%)
    ppermute x7, waiting for transfers between devices, shift(): lax.ppermute(x, 'ep', [(2 * z + s, 2 * to + s) for z, to in pairs for s i...  28.3 us
    ppermute x7, starting transfers between devices, shift(): lax.ppermute(x, 'ep', [(2 * z + s, 2 * to + s) for z, to in pairs for s i...  26.6 us
    ppermute x4, waiting for transfers between devices, on_device(): other.append(lax.ppermute(rows, 'ep', cross))  19.8 us
    all_to_all x1, waiting for transfers between devices, on_device(): marks = lax.all_to_all(mine, 'ep', split_axis=0, concat_axis=0, tiled=True)  17.5 us
    pallas_call x5, Pallas kernels, meet(): pl.pallas_call(body, in_specs=[ANYWHERE] * (len(blocks) + len(flat)) + [L...  15 us
    pallas_call x2, Pallas kernels, split_rows(): pl.pallas_call(body, grid=(parts // group,), in_specs=[pl.BlockSpec((grou...  12.5 us
    all_to_all x1, waiting for transfers between devices, on_device(): lax.all_to_all(sent, ('ep', 'dp'), split_axis=0, concat_axis=0, tiled=True)  11 us
    all_to_all x1, starting transfers between devices, on_device(): lax.all_to_all(message, 'ep', split_axis=0, concat_axis=0, tiled=True, ax...  8 us
  transfers between devices with their start and end apart: 15, of which 6 were waited for; matrix products, arithmetic and copies ran while one was open for 4% of the time, Pallas kernels for 19%

profile of v1, /device:TPU:0, one launch (start us, length us, event | category | flops | bytes accessed | tf_op | source)
XLA Modules:
  0.0 176.8 jit_solution(9653337300793190757)
XLA Ops:
  0.6 5.0 %collective-permute-start = (bf16[192,2880]{1,0:T(8,128)(2,1)}, bf16[192,2880]{1,0:T(8,128)(2,1)S(1)}, u32[]{:S(2)}, u32[]{:S(2)}) collective-permute-start(bf16[192,2880]{1,0:T(8,128)(2,1)} %block_ref.1), channel_id=1, source_target_pairs={{0,8},{4,12},{8,16},{12,20},{16,24},{20,28},{1,9},{5,13},{9,17},{1... | collective-permute-start | bytes 3317768 | tf_op jit(solution)/shard_map/ppermute | solution.py:319
  7.0 23.1 %collective-permute-done.refs_0_.refs_1_ = bf16[192,2880]{1,0:T(8,128)(2,1)S(1)} collective-permute-done((bf16[192,2880]{1,0:T(8,128)(2,1)}, bf16[192,2880]{1,0:T(8,128)(2,1)S(1)}, u32[]{:S(2)}, u32[]{:S(2)}) %collective-permute-start) | collective-permute-done | bytes 1105952 | tf_op jit(solution)/shard_map/ppermute | solution.py:319
  30.1 1.7 collective-permute-start.3
  31.8 5.1 %split_rows.2 = bf16[144,2880]{1,0:T(8,128)(2,1)} custom-call(bf16[1152,2880]{1,0:T(8,128)(2,1)} %bitcast.21), custom_call_target="tpu_custom_call" | custom-call | flops 106168320 | bytes 9953280 | tf_op jit(solution)/shard_map/split_rows/pallas_call | solution.py:57
  38.4 7.4 %split_rows.3 = (bf16[144,2880]{1,0:T(8,128)(2,1)}, bf16[144,2880]{1,0:T(8,128)(2,1)}, bf16[144,2880]{1,0:T(8,128)(2,1)}, bf16[144,2880]{1,0:T(8,128)(2,1)}, bf1...) custom-call(bf16[1152,2880]{1,0:T(8,128)(2,1)} %bitcast.22), custom_call_target="tpu_custom_call" | custom-call | flops 743178240 | bytes 9953280 | tf_op jit(solution)/shard_map/split_rows/pallas_call | solution.py:57
  49.1 9.7 %collective-permute-done.6.refs_4_ = bf16[144,2880]{1,0:T(8,128)(2,1)S(1)} collective-permute-done((bf16[144,2880]{1,0:T(8,128)(2,1)}, bf16[144,2880]{1,0:T(8,128)(2,1)S(1)}, u32[]{:S(2)}, u32[]{:S(2)}) %collective-permute-start.6) | collective-permute-done | bytes 829472 | tf_op jit(solution)/shard_map/ppermute | solution.py:315
  58.8 8.0 %collective-permute-start.8 = (bf16[144,2880]{1,0:T(8,128)(2,1)}, bf16[144,2880]{1,0:T(8,128)(2,1)}, u32[]{:S(2)}, u32[]{:S(2)}) collective-permute-start(bf16[144,2880]{1,0:T(8,128)(2,1)} %get-tuple-element.24.refs_3_), channel_id=1, source_target_pairs={{0,8},{4,12},{24,16},{28,20},{1,9},{5,13},{25,17},{29,21},{2,10},{... | collective-permute-start | bytes 2488328 | tf_op jit(solution)/shard_map/ppermute | solution.py:319
  66.8 10.2 %collective-permute-done.5.refs_6_ = bf16[144,2880]{1,0:T(8,128)(2,1)S(1)} collective-permute-done((bf16[144,2880]{1,0:T(8,128)(2,1)}, bf16[144,2880]{1,0:T(8,128)(2,1)S(1)}, u32[]{:S(2)}, u32[]{:S(2)}) %collective-permute-start.5) | collective-permute-done | bytes 829472 | tf_op jit(solution)/shard_map/ppermute | solution.py:315
  77.0 8.0 %collective-permute-start.7 = (bf16[144,2880]{1,0:T(8,128)(2,1)S(1)}, bf16[144,2880]{1,0:T(8,128)(2,1)}, u32[]{:S(2)}, u32[]{:S(2)}) collective-permute-start(bf16[144,2880]{1,0:T(8,128)(2,1)S(1)} %collective-permute-done.6.refs_4_), channel_id=1, source_target_pairs={{0,8},{4,12},{24,16},{28,20},{1,9},{5,13},{25,17},{29,21},{2,10},{... | collective-permute-start | bytes 2488328 | tf_op jit(solution)/shard_map/ppermute | solution.py:319
  88.1 3.4 %all-to-all-start = ((s32[8,8,4,192]{3,2,1,0:T(4,128)}), s32[8,8,4,192]{3,2,1,0:T(4,128)S(1)}, u32[]{:S(2)}, u32[]{:S(2)}) async-start(s32[8,8,4,192]{3,2,1,0:T(4,128)} %slot_marks.1), calls=%async_computation | async-start | bytes 524288 | tf_op jit(solution)/shard_map/all_to_all | solution.py:337
  94.2 2.4 %router.1 = (f32[32,192]{1,0:T(8,128)}, f32[32,192]{1,0:T(8,128)}, f32[1,32]{1,0:T(1,128)}) custom-call(bf16[32,2880]{1,0:T(8,128)(2,1)} %bitcast.24, bf16[192,2880]{1,0:T(8,128)(2,1)} %tokens_ref.1, f32[32,1]{1,0:T(8,128)} %copy.17.bias_ref, s32[8,4,192]{2,1,0:T(4,128)} %slice_bitcast_fusion.marks_ref), custom_call_target="tpu_custom_call" | custom-call | flops 35389440 | bytes 1290240 | tf_op jit(solution)/shard_map/router/pallas_call | solution.py:115
  96.6 17.5 %all-to-all-done.refs_7_.refs_4_.refs_3_.marks_ref = s32[8,8,4,192]{3,2,1,0:T(4,128)S(1)} async-done(((s32[8,8,4,192]{3,2,1,0:T(4,128)}), s32[8,8,4,192]{3,2,1,0:T(4,128)S(1)}, u32[]{:S(2)}, u32[]{:S(2)}) %all-to-all-start) | async-done | bytes 196640 | tf_op jit(solution)/shard_map/all_to_all | solution.py:337
  115.0 3.2 %all-to-all-start.2 = ((f32[4,1,32]{2,1,0:T(1,128)}), f32[4,1,32]{2,1,0:T(1,128)S(1)}, u32[]{:S(2)}, u32[]{:S(2)}) async-start(f32[4,1,32]{2,1,0:T(1,128)} %broadcast_in_dim.24), calls=%async_computation.2 | async-start | bytes 4096 | tf_op jit(solution)/shard_map/all_to_all | solution.py:339
  118.8 4.2 %meet.5.refs_8_ = f32[4,8,192]{2,1,0:T(8,128)} custom-call(bf16[192,2880]{1,0:T(8,128)(2,1)} %copy-done.1, bf16[192,2880]{1,0:T(8,128)(2,1)} %block_ref.1, bf16[192,2880]{1,0:T(8,128)(2,1)} %copy-done.2, bf16[144,2880]{1,0:T(8,128)(2,1)} %get-tuple-element.24.refs_3_, bf16[144,2880]{1,0:T(8,128)(2,1)} %copy-done.3, ...), custom_call_target="tpu_custom_call", output_to_operand_aliasing={{}: (8, {})} | custom-call | flops 637009920 | bytes 6635520 | tf_op jit(solution)/shard_map/meet/pallas_call | solution.py:195
  123.1 4.0 %meet.6.refs_5_ = f32[4,8,192]{2,1,0:T(8,128)} custom-call(bf16[192,2880]{1,0:T(8,128)(2,1)} %collective-permute-done.3.refs_0_, bf16[192,2880]{1,0:T(8,128)(2,1)} %copy-done.1, bf16[192,2880]{1,0:T(8,128)(2,1)} %block_ref.1, bf16[192,2880]{1,0:T(8,128)(2,1)} %copy-done.2, ...), custom_call_target="tpu_custom_call", output_to_operand_aliasing={{}: (8, {})} | custom-call | flops 318504960 | bytes 3317760 | tf_op jit(solution)/shard_map/meet/pallas_call | solution.py:195
  127.1 3.6 %meet.7 = f32[4,8,192]{2,1,0:T(8,128)} custom-call(bf16[192,2880]{1,0:T(8,128)(2,1)} %copy-done.1, bf16[192,2880]{1,0:T(8,128)(2,1)} %block_ref.1, bf16[192,2880]{1,0:T(8,128)(2,1)} %copy-done.2, bf16[144,2880]{1,0:T(8,128)(2,1)} %collective-permute-done.2.refs_3_, s32[8,8,4,192]{3,2,1,0:T(4,128)} %copy-done, ...), custom_call_target="tpu_custom_call", output_to_operand_aliasing={{}: (5, {})} | custom-call | flops 159252480 | bytes 1658880 | tf_op jit(solution)/shard_map/meet/pallas_call | solution.py:195
  130.7 8.0 %all-to-all-start.1 = ((f32[4,8,192]{2,1,0:T(8,128)}), f32[4,8,192]{2,1,0:T(8,128)S(1)}, u32[]{:S(2)}, u32[]{:S(2)}) async-start(f32[4,8,192]{2,1,0:T(8,128)} %meet.7), calls=%async_computation.1 | async-start | bytes 65536 | tf_op jit(solution)/shard_map/all_to_all | solution.py:369
  141.0 1.6 meet.9
  144.8 2.7 %last_dots.1.late_ref = f32[4,192]{1,0:T(4,128)} custom-call(bf16[192,2880]{1,0:T(8,128)(2,1)} %block_ref.1, bf16[1,144,2880]{2,1,0:T(8,128)(2,1)} %bitcast.23, s32[8,8,4,192]{3,2,1,0:T(4,128)} %copy-done), custom_call_target="tpu_custom_call" | custom-call | flops 159252480 | bytes 1935360 | tf_op jit(solution)/shard_map/last_dots/pallas_call | solution.py:226
  147.5 5.2 %collective-permute-done.9.guest_ref = f32[1,8,192]{2,1,0:T(8,128)S(1)} collective-permute-done((f32[1,8,192]{2,1,0:T(8,128)}, f32[1,8,192]{2,1,0:T(8,128)S(1)}, u32[]{:S(2)}, u32[]{:S(2)}) %collective-permute-start.9) | collective-permute-done | bytes 6176 | tf_op jit(solution)/shard_map/ppermute | solution.py:319
  153.3 2.6 %finish.1 = (bf16[32,192]{1,0:T(8,128)(2,1)}, f32[32,4,768]{2,1,0:T(4,128)}) custom-call(f32[1]{0:T(128)S(6)} %copy.23.scale_ref, f32[4,8,192]{2,1,0:T(8,128)} %copy-done.7, f32[1,8,192]{2,1,0:T(8,128)} %copy-done.10, f32[4,192]{1,0:T(4,128)} %last_dots.1.late_ref, f32[32,192]{1,0:T(8,128)} %get-tuple-element.30.mix_ref, ...), custom_call_target="tpu_custom_call" | custom-call | flops 35389440 | bytes 1474560 | tf_op jit(solution)/shard_map/finish/pallas_call | solution.py:278
  155.9 4.5 %all-to-all-start.3 = ((f32[32,4,768]{2,1,0:T(4,128)}), f32[32,4,768]{2,1,0:T(4,128)S(1)}, u32[]{:S(2)}, u32[]{:S(2)}) async-start(f32[32,4,768]{2,1,0:T(4,128)} %get-tuple-element.34), calls=%async_computation.3 | async-start | bytes 786432 | tf_op jit(solution)/shard_map/all_to_all | solution.py:383
  160.5 2.2 %convolution_convert_fusion = bf16[192,2880]{1,0:T(8,128)(2,1)} fusion(bf16[32,192]{1,0:T(8,128)(2,1)} %get-tuple-element.33, bf16[2880,32]{0,1:T(8,128)(2,1)S(1)} %copy-done.6), kind=kOutput, calls=%fused_computation | convolution fusion | flops 35942400 | bytes 1302528 | tf_op jit(solution)/shard_map/dot_general | solution.py:380
  162.7 11.0 %all-to-all-done.3 = f32[32,4,768]{2,1,0:T(4,128)S(1)} async-done(((f32[32,4,768]{2,1,0:T(4,128)}), f32[32,4,768]{2,1,0:T(4,128)S(1)}, u32[]{:S(2)}, u32[]{:S(2)}) %all-to-all-start.3) | async-done | bytes 393248 | tf_op jit(solution)/shard_map/all_to_all | solution.py:383
  (53 shorter events, 19.2 us)
Async XLA Ops:
  0.6 29.4 %collective-permute-start = (bf16[192,2880]{1,0:T(8,128)(2,1)}, bf16[192,2880]{1,0:T(8,128)(2,1)S(1)}, u32[]{:S(2)}, u32[]{:S(2)}) collective-permute-start(bf16[192,2880]{1,0:T(8,128)(2,1)} %block_ref.1), channel_id=1, source_target_pairs={{0,8},{4,12},{8,16},{12,20},{16,24},{20,28},{1,9},{5,13},{9,17},{1... | collective-permute-start | bytes 3317768 | tf_op jit(solution)/shard_map/ppermute | solution.py:319
  5.7 40.6 %collective-permute-start.1 = (bf16[192,2880]{1,0:T(8,128)(2,1)}, bf16[192,2880]{1,0:T(8,128)(2,1)S(1)}, u32[]{:S(2)}, u32[]{:S(2)}) collective-permute-start(bf16[192,2880]{1,0:T(8,128)(2,1)} %block_ref.1), channel_id=1, source_target_pairs={{8,0},{12,4},{16,8},{20,12},{24,16},{28,20},{9,1},{13,5},{17,9},{2... | collective-permute-start | bytes 3317768 | tf_op jit(solution)/shard_map/ppermute | solution.py:319
  30.1 6.8 %copy-start.1 = (bf16[192,2880]{1,0:T(8,128)(2,1)}, bf16[192,2880]{1,0:T(8,128)(2,1)S(1)}, u32[]{:S(2)}) copy-start(bf16[192,2880]{1,0:T(8,128)(2,1)S(1)} %collective-permute-done.refs_0_.refs_1_) | copy-start | bytes 3317764
  30.1 54.9 %collective-permute-start.3 = (bf16[192,2880]{1,0:T(8,128)(2,1)S(1)}, bf16[192,2880]{1,0:T(8,128)(2,1)}, u32[]{:S(2)}, u32[]{:S(2)}) collective-permute-start(bf16[192,2880]{1,0:T(8,128)(2,1)S(1)} %collective-permute-done.refs_0_.refs_1_), channel_id=1, source_target_pairs={{8,16},{12,20},{16,24},{20,28},{9,17},{13,21},{17,25},{21,29},{10,... | collective-permute-start | bytes 3317768 | tf_op jit(solution)/shard_map/ppermute | solution.py:319
  36.9 54.6 %copy-start.11 = (f32[32]{0:T(128)S(1)}, f32[32]{0:T(128)}, u32[]{:S(2)}) copy-start(f32[32]{0:T(128)} %param.12) | copy-start | bytes 388
  36.9 21.9 %collective-permute-start.6 = (bf16[144,2880]{1,0:T(8,128)(2,1)}, bf16[144,2880]{1,0:T(8,128)(2,1)S(1)}, u32[]{:S(2)}, u32[]{:S(2)}) collective-permute-start(bf16[144,2880]{1,0:T(8,128)(2,1)} %split_rows.2), channel_id=1, source_target_pairs={{0,4},{4,0},{8,12},{12,8},{16,20},{20,16},{24,28},{28,24},{1,5},{5... | collective-permute-start | bytes 2488328 | tf_op jit(solution)/shard_map/ppermute | solution.py:315
  45.8 31.2 %collective-permute-start.5 = (bf16[144,2880]{1,0:T(8,128)(2,1)}, bf16[144,2880]{1,0:T(8,128)(2,1)S(1)}, u32[]{:S(2)}, u32[]{:S(2)}) collective-permute-start(bf16[144,2880]{1,0:T(8,128)(2,1)} %get-tuple-element.21), channel_id=1, source_target_pairs={{0,4},{4,0},{8,12},{12,8},{16,20},{20,16},{24,28},{28,24},{1,5},{5... | collective-permute-start | bytes 2488328 | tf_op jit(solution)/shard_map/ppermute | solution.py:315
  46.3 68.0 %copy-start.2 = (bf16[192,2880]{1,0:T(8,128)(2,1)}, bf16[192,2880]{1,0:T(8,128)(2,1)S(1)}, u32[]{:S(2)}) copy-start(bf16[192,2880]{1,0:T(8,128)(2,1)S(1)} %collective-permute-done.1.refs_2_.refs_3_) | copy-start | bytes 3317764
  46.3 76.8 %collective-permute-start.4 = (bf16[192,2880]{1,0:T(8,128)(2,1)S(1)}, bf16[192,2880]{1,0:T(8,128)(2,1)}, u32[]{:S(2)}, u32[]{:S(2)}) collective-permute-start(bf16[192,2880]{1,0:T(8,128)(2,1)S(1)} %collective-permute-done.1.refs_2_.refs_3_), channel_id=1, source_target_pairs={{8,0},{12,4},{16,8},{20,12},{9,1},{13,5},{17,9},{21,13},{10,2},{14... | collective-permute-start | bytes 3317768 | tf_op jit(solution)/shard_map/ppermute | solution.py:319
  47.6 79.5 %collective-permute-start.2 = (bf16[144,2880]{1,0:T(8,128)(2,1)}, bf16[144,2880]{1,0:T(8,128)(2,1)}, u32[]{:S(2)}, u32[]{:S(2)}) collective-permute-start(bf16[144,2880]{1,0:T(8,128)(2,1)} %get-tuple-element.20), channel_id=1, source_target_pairs={{0,4},{4,0},{8,12},{12,8},{16,20},{20,16},{24,28},{28,24},{1,5},{5... | collective-permute-start | bytes 2488328 | tf_op jit(solution)/shard_map/ppermute | solution.py:315
  58.8 55.5 %copy-start.3 = (bf16[144,2880]{1,0:T(8,128)(2,1)}, bf16[144,2880]{1,0:T(8,128)(2,1)S(1)}, u32[]{:S(2)}) copy-start(bf16[144,2880]{1,0:T(8,128)(2,1)S(1)} %collective-permute-done.6.refs_4_) | copy-start | bytes 2488324
  58.8 79.9 %collective-permute-start.8 = (bf16[144,2880]{1,0:T(8,128)(2,1)}, bf16[144,2880]{1,0:T(8,128)(2,1)}, u32[]{:S(2)}, u32[]{:S(2)}) collective-permute-start(bf16[144,2880]{1,0:T(8,128)(2,1)} %get-tuple-element.24.refs_3_), channel_id=1, source_target_pairs={{0,8},{4,12},{24,16},{28,20},{1,9},{5,13},{25,17},{29,21},{2,10},{... | collective-permute-start | bytes 2488328 | tf_op jit(solution)/shard_map/ppermute | solution.py:319
  77.0 8.0 %copy-start.4 = (bf16[144,2880]{1,0:T(8,128)(2,1)}, bf16[144,2880]{1,0:T(8,128)(2,1)S(1)}, u32[]{:S(2)}) copy-start(bf16[144,2880]{1,0:T(8,128)(2,1)S(1)} %collective-permute-done.5.refs_6_) | copy-start | bytes 2488324
  77.0 64.0 %collective-permute-start.7 = (bf16[144,2880]{1,0:T(8,128)(2,1)S(1)}, bf16[144,2880]{1,0:T(8,128)(2,1)}, u32[]{:S(2)}, u32[]{:S(2)}) collective-permute-start(bf16[144,2880]{1,0:T(8,128)(2,1)S(1)} %collective-permute-done.6.refs_4_), channel_id=1, source_target_pairs={{0,8},{4,12},{24,16},{28,20},{1,9},{5,13},{25,17},{29,21},{2,10},{... | collective-permute-start | bytes 2488328 | tf_op jit(solution)/shard_map/ppermute | solution.py:319
  85.0 58.9 %collective-permute-start.10 = (bf16[144,2880]{1,0:T(8,128)(2,1)}, bf16[144,2880]{1,0:T(8,128)(2,1)S(1)}, u32[]{:S(2)}, u32[]{:S(2)}) collective-permute-start(bf16[144,2880]{1,0:T(8,128)(2,1)} %get-tuple-element.28), channel_id=1, source_target_pairs={{0,4},{4,0},{8,12},{12,8},{16,20},{20,16},{24,28},{28,24},{1,5},{5... | collective-permute-start | bytes 2488328 | tf_op jit(solution)/shard_map/ppermute | solution.py:315
  88.1 26.1 %all-to-all-start = ((s32[8,8,4,192]{3,2,1,0:T(4,128)}), s32[8,8,4,192]{3,2,1,0:T(4,128)S(1)}, u32[]{:S(2)}, u32[]{:S(2)}) async-start(s32[8,8,4,192]{3,2,1,0:T(4,128)} %slot_marks.1), calls=%async_computation | async-start | bytes 524288 | tf_op jit(solution)/shard_map/all_to_all | solution.py:337
  114.1 4.7 %copy-start = (s32[8,8,4,192]{3,2,1,0:T(4,128)}, s32[8,8,4,192]{3,2,1,0:T(4,128)S(1)}, u32[]{:S(2)}) copy-start(s32[8,8,4,192]{3,2,1,0:T(4,128)S(1)} %all-to-all-done.refs_7_.refs_4_.refs_3_.marks_ref) | copy-start | bytes 589828
  115.0 15.8 %all-to-all-start.2 = ((f32[4,1,32]{2,1,0:T(1,128)}), f32[4,1,32]{2,1,0:T(1,128)S(1)}, u32[]{:S(2)}, u32[]{:S(2)}) async-start(f32[4,1,32]{2,1,0:T(1,128)} %broadcast_in_dim.24), calls=%async_computation.2 | async-start | bytes 4096 | tf_op jit(solution)/shard_map/all_to_all | solution.py:339
  130.7 10.2 %copy-start.8 = (f32[4,1,32]{2,1,0:T(1,128)}, f32[4,1,32]{2,1,0:T(1,128)S(1)}, u32[]{:S(2)}) copy-start(f32[4,1,32]{2,1,0:T(1,128)S(1)} %all-to-all-done.2) | copy-start | bytes 1540
  130.7 21.9 %all-to-all-start.1 = ((f32[4,8,192]{2,1,0:T(8,128)}), f32[4,8,192]{2,1,0:T(8,128)S(1)}, u32[]{:S(2)}, u32[]{:S(2)}) async-start(f32[4,8,192]{2,1,0:T(8,128)} %meet.7), calls=%async_computation.1 | async-start | bytes 65536 | tf_op jit(solution)/shard_map/all_to_all | solution.py:369
  142.6 10.1 %collective-permute-start.9 = (f32[1,8,192]{2,1,0:T(8,128)}, f32[1,8,192]{2,1,0:T(8,128)S(1)}, u32[]{:S(2)}, u32[]{:S(2)}) collective-permute-start(f32[1,8,192]{2,1,0:T(8,128)} %meet.9), channel_id=1, source_target_pairs={{8,24},{12,28},{16,0},{20,4},{9,25},{13,29},{17,1},{21,5},{10,26},... | collective-permute-start | bytes 18440 | tf_op jit(solution)/shard_map/ppermute | solution.py:319
  147.5 13.0 %copy-start.9 = (f32[4,1,32]{2,1,0:T(1,128)S(1)}, f32[4,1,32]{2,1,0:T(1,128)}, u32[]{:S(2)}) copy-start(f32[4,1,32]{2,1,0:T(1,128)} %copy-done.8) | copy-start | bytes 1540
  147.5 13.0 %copy-start.6 = (bf16[2880,32]{0,1:T(8,128)(2,1)S(1)}, bf16[2880,32]{0,1:T(8,128)(2,1)}, u32[]{:S(2)}) copy-start(bf16[2880,32]{0,1:T(8,128)(2,1)} %param.11) | copy-start | bytes 552964
  155.9 17.8 %all-to-all-start.3 = ((f32[32,4,768]{2,1,0:T(4,128)}), f32[32,4,768]{2,1,0:T(4,128)S(1)}, u32[]{:S(2)}, u32[]{:S(2)}) async-start(f32[32,4,768]{2,1,0:T(4,128)} %get-tuple-element.34), calls=%async_computation.3 | async-start | bytes 786432 | tf_op jit(solution)/shard_map/all_to_all | solution.py:383
  (3 other events, 2.1 us)

commit v2 on v1

--- a/solution.py
+++ b/solution.py
@@ -124,33 +124,78 @@
     )(weight, tokens, bias, marks)
 
 
-def slot_dots(rows, block, marks, exp_dev, put):
+def offsets(mark, exp_dev):
+    begin, total = [], jnp.zeros((1, 1), jnp.int32)
+    for e in range(exp_dev):
+        begin.append(total)
+        total = total + jnp.sum((mark[e:e + 1] >= 0).astype(jnp.int32), axis=1, keepdims=True)
+    return begin + [total]
+
+
+def pack_rows(chunks, places, marks, exp_dev, size):
+    entries, width = chunks[0].shape
+    length, cap = marks.shape[0] // 2, entries // exp_dev
+
+    def body(*refs):
+        chunk_refs, marks_ref, outs = refs[:len(chunks)], refs[len(chunks)], refs[len(chunks) + 1:]
+        side, place, _ = spot(length)
+        row = lax.broadcasted_iota(jnp.int32, (size, entries), 0)
+        entry = lax.broadcasted_iota(jnp.int32, (size, entries), 1)
+        for chunk, n, out in zip(chunk_refs, places, outs):
+            mark = marks_ref[2 * source_at(length, n) + 1 - side, 2 * place + side]
+            begin = offsets(mark, exp_dev)
+            sel = jnp.zeros((size, entries), F32)
+            for e in range(exp_dev):
+                slot = entry - e * cap
+                used = (slot >= 0) & (slot < begin[e + 1] - begin[e])
+                sel = jnp.where(used & (row == begin[e] + slot), 1.0, sel)
+            out[...] = jnp.dot(sel.astype(BF16), chunk[...], preferred_element_type=F32).astype(BF16)
+
+    return pl.pallas_call(
+        body,
+        in_specs=[LOCAL] * (len(chunks) + 1),
+        out_specs=[LOCAL] * len(chunks),
+        out_shape=[jax.ShapeDtypeStruct((size, width), BF16)] * len(chunks),
+        cost_estimate=pl.CostEstimate(
+            flops=2 * len(chunks) * size * entries * width, bytes_accessed=4 * len(chunks) * entries * width, transcendentals=0
+        ),
+        name="pack_rows",
+    )(*chunks, marks)
+
+
+def slot_dots(rows, block, marks, exp_dev, entries, put):
     kinds, count, width = rows.shape
-    tok, cap = block.shape[0], count // exp_dev
+    cap = entries // exp_dev
     if count % 16 == 0:
         full = lax.dot_general(rows[...].reshape(kinds * count, width), block[...], NT, preferred_element_type=F32)
         full = [full[k * count:(k + 1) * count] for k in range(kinds)]
     else:
         full = [lax.dot_general(rows[k], block[...], NT, preferred_element_type=F32) for k in range(kinds)]
-    slots = lax.broadcasted_iota(jnp.int32, (cap, tok), 0)
     for kind, mark in enumerate(marks):
+        begin = offsets(mark, exp_dev)
         for e in range(exp_dev):
-            part = jnp.where(slots == mark[e:e + 1], full[kind][e * cap:(e + 1) * cap], 0.0)
-            put(kind, e, jnp.sum(part, axis=0, keepdims=True))
-
-
-def meet(blocks, jobs, marks, message, exp_dev):
+            at = mark[e:e + 1]
+            part = full[kind][e * cap:(e + 1) * cap]
+            if count != entries:
+                at = jnp.where(at >= 0, at + begin[e], -1)
+                part = full[kind]
+            slots = lax.broadcasted_iota(jnp.int32, part.shape, 0)
+            put(kind, e, jnp.sum(jnp.where(slots == at, part, 0.0), axis=0, keepdims=True))
+
+
+def meet(blocks, jobs, marks, answers, exp_dev, entries):
     tok, width = blocks[0].shape
     length = marks.shape[0] // 2
     flat = [r for job in jobs for r in job[0]]
-    count = flat[0].shape[0]
     most = max(len(job[0]) for job in jobs)
     first = [sum(len(job[0]) for job in jobs[:n]) for n in range(len(jobs))]
 
     def body(*refs):
         block_refs, refs = refs[:len(blocks)], refs[len(blocks):]
         row_refs, refs = refs[:len(flat)], refs[len(flat):]
-        marks_ref, in_ref, out_ref, held, rows_held, block_sem, row_sem = refs
+        marks_ref, refs = refs[0], refs[1:]
+        in_refs, refs = refs[:len(answers)], refs[len(answers):]
+        out_refs, (held, rows_held, block_sem, row_sem) = refs[:len(answers)], refs[len(answers):]
         side = spot(length)[0]
         plans = [job[2]() for job in jobs]
 
@@ -158,7 +203,9 @@
             return (plans[n][2] >= 0) & (plans[n][2] < len(blocks))
 
         def rows_copy(n, k):
-            return pltpu.make_async_copy(row_refs[first[n] + k], rows_held.at[n % 2, k], row_sem.at[n % 2, k])
+            source = row_refs[first[n] + k]
+            to = rows_held.at[n % 2, k, pl.ds(0, source.shape[0])] if source.shape[0] != entries else rows_held.at[n % 2, k]
+            return pltpu.make_async_copy(source, to, row_sem.at[n % 2, k])
 
         def start(n):
             for i, block in enumerate(block_refs):
@@ -172,7 +219,8 @@
                     rows_copy(n, k).start()
 
         start(0)
-        out_ref[...] = in_ref[...]
+        for in_ref, out_ref in zip(in_refs, out_refs):
+            out_ref[...] = in_ref[...]
         for n in range(len(jobs)):
             if n + 1 < len(jobs):
                 start(n + 1)
@@ -187,31 +235,36 @@
 
                 def put(k, e, value):
                     line = jobs[n][3] + kinds[k] * exp_dev + e
-                    out_ref[pl.ds(target, 1), line:line + 1, :] = value[None]
+                    out_refs[jobs[n][4]][pl.ds(target, 1), line:line + 1, :] = value[None]
 
                 each = [marks_ref[2 * source + side, 2 * column + (1 - side if kind else side)] for kind in kinds]
-                slot_dots(rows_held.at[n % 2, pl.ds(0, len(rows))], held.at[n % 2], each, exp_dev, put)
-
-    return pl.pallas_call(
-        body,
-        in_specs=[ANYWHERE] * (len(blocks) + len(flat)) + [LOCAL] * 2,
-        out_specs=LOCAL,
-        out_shape=jax.ShapeDtypeStruct(message.shape, F32),
-        input_output_aliases={1 + len(blocks) + len(flat): 0},
+                count = rows[0].shape[0]
+                lines = rows_held.at[n % 2, pl.ds(0, len(rows))]
+                if count != entries:
+                    lines = rows_held.at[n % 2, pl.ds(0, len(rows)), pl.ds(0, count)]
+                slot_dots(lines, held.at[n % 2], each, exp_dev, entries, put)
+
+    given = len(blocks) + len(flat) + 1
+    return pl.pallas_call(
+        body,
+        in_specs=[ANYWHERE] * (given - 1) + [LOCAL] * (1 + len(answers)),
+        out_specs=[LOCAL] * len(answers),
+        out_shape=[jax.ShapeDtypeStruct(x.shape, F32) for x in answers],
+        input_output_aliases={given + i: i for i in range(len(answers))},
         scratch_shapes=[
             pltpu.VMEM((2, tok, width), BF16),
-            pltpu.VMEM((2, most, count, width), BF16),
+            pltpu.VMEM((2, most, entries, width), BF16),
             pltpu.SemaphoreType.DMA((2,)),
             pltpu.SemaphoreType.DMA((2, most)),
         ],
         cost_estimate=pl.CostEstimate(
-            flops=2 * len(flat) * tok * count * width, bytes_accessed=4 * len(flat) * count * width, transcendentals=0
+            flops=2 * len(flat) * tok * entries * width, bytes_accessed=4 * len(flat) * entries * width, transcendentals=0
         ),
         name="meet",
-    )(*blocks, *flat, marks, message)
-
-
-def last_dots(block, rows, marks, exp_dev):
+    )(*blocks, *flat, marks, *answers)
+
+
+def last_dots(block, rows, marks, exp_dev, entries):
     tok, length = block.shape[0], marks.shape[0] // 2
 
     def body(block_ref, rows_ref, marks_ref, out_ref):
@@ -221,7 +274,7 @@
             out_ref[e:e + 1, :] = value
 
         mark = marks_ref[2 * place + side, 2 * place + 1 - side]
-        slot_dots(rows_ref, block_ref, [mark], exp_dev, put)
+        slot_dots(rows_ref, block_ref, [mark], exp_dev, entries, put)
 
     return pl.pallas_call(
         body,
@@ -310,6 +363,15 @@
     block = out_grad
     rest = list(split_rows(table, [(n, True) for n in range(1, length)] + [(n, False) for n in range(length)], ep))
     leaving, own = leaving + rest[:length - 1], rest[length - 1:]
+
+    chosen, _ = lax.optimization_barrier((indices.T, rest[0]))
+    mine = slot_marks(chosen, ep, exp_dev)
+    marks = lax.all_to_all(mine, "ep", split_axis=0, concat_axis=0, tiled=True)
+    counts = jnp.sum((marks >= 0).astype(F32), axis=(0, 3)).reshape(1, experts)
+    counts = lax.all_to_all(jnp.broadcast_to(counts, (dp, experts)), "dp", split_axis=0, concat_axis=0, tiled=True)
+
+    size = min(entries, -(-capacity * (exp_dev - 1) // 16) * 16)
+    leaving[-2:] = pack_rows(leaving[-2:], [length - 2, length - 1], marks, exp_dev, size)
     other = []
     for rows in leaving:
         other.append(lax.ppermute(rows, "ep", cross))
@@ -332,12 +394,6 @@
         for rows in (own, other):
             guests[-1].append(shift(rows[length - 1 - d], *moves))
 
-    chosen, _ = lax.optimization_barrier((indices.T, rest[0]))
-    mine = slot_marks(chosen, ep, exp_dev)
-    marks = lax.all_to_all(mine, "ep", split_axis=0, concat_axis=0, tiled=True)
-    counts = jnp.sum((marks >= 0).astype(F32), axis=(0, 3)).reshape(1, experts)
-    counts = lax.all_to_all(jnp.broadcast_to(counts, (dp, experts)), "dp", split_axis=0, concat_axis=0, tiled=True)
-
     tokens, _ = lax.optimization_barrier((tokens, rest[0]))
     probability, mix, prob_sums = router(router_weight.T, tokens, router_bias[:, None], mine[0])
 
@@ -347,7 +403,7 @@
             source = source_at(length, n)
             return source, place, source - place + hops, source
 
-        return [(own, other)[kind][n] for kind in kinds], kinds, plan, 0
+        return [(own, other)[kind][n] for kind in kinds], kinds, plan, 0, 0
 
     def guest_job(i, kind):
         def plan():
@@ -355,23 +411,23 @@
             column = place + jnp.where(low, -i, i)
             source = place + jnp.where(low, reach, -reach)
             there = (column >= 0) & (column < length)
-            which = jnp.where(there, jnp.where(low, 1, 0), -1)
+            which = jnp.where(there, jnp.where(low, 2 * reach, 0), -1)
             return source, jnp.clip(column, 0, length - 1), which, 0
 
-        return [guests[i - 1][kind]], (kind,), plan, 2 * (i - 1) * exp_dev
+        return [guests[i - 1][kind]], (kind,), plan, 2 * (i - 1) * exp_dev, 1
 
     message = jnp.zeros((length, 2 * exp_dev, tok), F32)
+    guest = jnp.zeros((1, 2 * exp_dev * far, tok), F32)
     near = [job(0, (0, 1), 1), job(length - 2, (0,), 1), job(length - 1, (0,), 1)]
-    message = meet(blocks[reach - 1:reach + 2], near, marks, message, exp_dev)
-    message = meet(blocks, [job(n, (0, 1), reach) for n in range(1, length - 2)], marks, message, exp_dev)
-    message = meet(blocks[reach - 1:reach + 2], [job(length - 2, (1,), 1)], marks, message, exp_dev)
+    message, = meet(blocks[reach - 1:reach + 2], near, marks, [message], exp_dev, entries)
+    with_guests = [job(n, (0, 1), reach) for n in range(1, length - 2)] + [guest_job(i, 0) for i in range(1, far + 1)]
+    message, guest = meet(blocks, with_guests, marks, [message, guest], exp_dev, entries)
+    late_jobs = [job(length - 2, (1,), reach)] + [guest_job(i, 1) for i in range(1, far + 1)]
+    message, guest = meet(blocks, late_jobs, marks, [message, guest], exp_dev, entries)
     rows_of = [[2 * z + s for z in range(length)] for s in range(2)]
     got = lax.all_to_all(message, "ep", split_axis=0, concat_axis=0, tiled=True, axis_index_groups=rows_of)
-    guest = jnp.zeros((1, 2 * exp_dev * far, tok), F32)
-    for kind in range(2):
-        guest = meet(blocks[::2 * reach], [guest_job(i, kind) for i in range(1, far + 1)], marks, guest, exp_dev)
     guest = shift(guest, (lambda z: 0 < z < reach, reach), (lambda z: reach <= z < length - 1, -reach))
-    late = last_dots(out_grad, other[length - 1], marks, exp_dev)
+    late = last_dots(out_grad, other[length - 1], marks, exp_dev, entries)
 
     share = 1.0 / (token_total * indices.shape[1])
     logit_grad, sent = finish(

time: 178 us -> 137 us (0.77)
  waiting for transfers between devices: 76.7 us -> 39.9 us
  starting transfers between devices: 50.9 us -> 45.9 us
    ppermute x7, waiting for transfers between devices: 28.3 us -> 7.99 us  [shift(): lax.ppermute(x, 'ep', [(2 * z + s, 2 * to + s) for z, to in pairs for s i...]
    ppermute x4, waiting for transfers between devices: 19.8 us -> 1.44 us  [on_device(): other.append(lax.ppermute(rows, 'ep', cross))]
    ppermute x7, starting transfers between devices: 26.6 us -> 20.9 us  [shift(): lax.ppermute(x, 'ep', [(2 * z + s, 2 * to + s) for z, to in pairs for s i...]
    all_to_all x1, starting transfers between devices: 3.41 us -> 8.13 us  [on_device(): marks = lax.all_to_all(mine, 'ep', split_axis=0, concat_axis=0, tiled=True)]
    all_to_all x1, starting transfers between devices: 8 us -> 3.94 us  [on_device(): lax.all_to_all(message, 'ep', split_axis=0, concat_axis=0, tiled=True, ax...]
    all_to_all x1, waiting for transfers between devices: 17.5 us -> 19.4 us  [on_device(): marks = lax.all_to_all(mine, 'ep', split_axis=0, concat_axis=0, tiled=True)]
    pallas_call x5 -> x4, Pallas kernels: 15 us -> 15 us  [the longest x3 11.9 us: meet(): pl.pallas_call(body, in_specs=[ANYWHERE] * (given - 1) + [LOCAL] * (1 + l...]
  transfers between devices with their start and end apart: 15 -> 15, of which waited for: 6 -> 6; matrix products, arithmetic and copies ran while one was open for 4% -> 5% of each run, Pallas kernels for 19% -> 25%
where the time goes in v2:
time: 137 us; the launch traced here: 136 us
  starting transfers between devices  45.9 us (34%)
  waiting for transfers between devices  39.9 us (29%)
  Pallas kernels  36.7 us (27%)
  local copies, waits for them, and re-layouts  5.29 us (4%)
  between operations  3.23 us (2%)
  other arithmetic  2.49 us (2%)
  matrix products  2.2 us (2%)
    ppermute x7, starting transfers between devices, shift(): lax.ppermute(x, 'ep', [(2 * z + s, 2 * to + s) for z, to in pairs for s i...  20.9 us
    all_to_all x1, waiting for transfers between devices, on_device(): marks = lax.all_to_all(mine, 'ep', split_axis=0, concat_axis=0, tiled=True)  19.4 us
    pallas_call x2, Pallas kernels, split_rows(): pl.pallas_call(body, grid=(parts // group,), in_specs=[pl.BlockSpec((grou...  12.5 us
    pallas_call x3, Pallas kernels, meet(): pl.pallas_call(body, in_specs=[ANYWHERE] * (given - 1) + [LOCAL] * (1 + l...  11.9 us
    all_to_all x1, waiting for transfers between devices, on_device(): lax.all_to_all(sent, ('ep', 'dp'), split_axis=0, concat_axis=0, tiled=True)  11 us
    all_to_all x1, starting transfers between devices, on_device(): marks = lax.all_to_all(mine, 'ep', split_axis=0, concat_axis=0, tiled=True)  8.13 us
    ppermute x7, waiting for transfers between devices, shift(): lax.ppermute(x, 'ep', [(2 * z + s, 2 * to + s) for z, to in pairs for s i...  7.99 us
    all_to_all x1, starting transfers between devices, on_device(): lax.all_to_all(sent, ('ep', 'dp'), split_axis=0, concat_axis=0, tiled=True)  5.72 us
  transfers between devices with their start and end apart: 15, of which 6 were waited for; matrix products, arithmetic and copies ran while one was open for 5% of the time, Pallas kernels for 25%

profile of v2, /device:TPU:0, one launch (start us, length us, event | category | flops | bytes accessed | tf_op | source)
XLA Modules:
  0.0 135.7 jit_solution(10981878268874412812)
XLA Ops:
  0.6 5.0 %collective-permute-start = (bf16[192,2880]{1,0:T(8,128)(2,1)}, bf16[192,2880]{1,0:T(8,128)(2,1)S(1)}, u32[]{:S(2)}, u32[]{:S(2)}) collective-permute-start(bf16[192,2880]{1,0:T(8,128)(2,1)} %block_ref.1), channel_id=1, source_target_pairs={{0,8},{4,12},{8,16},{12,20},{16,24},{20,28},{1,9},{5,13},{9,17},{1... | collective-permute-start | bytes 3317768 | tf_op jit(solution)/shard_map/ppermute | solution.py:381
  7.0 5.1 %split_rows.2 = bf16[144,2880]{1,0:T(8,128)(2,1)} custom-call(bf16[1152,2880]{1,0:T(8,128)(2,1)} %bitcast.21), custom_call_target="tpu_custom_call" | custom-call | flops 106168320 | bytes 9953280 | tf_op jit(solution)/shard_map/split_rows/pallas_call | solution.py:57
  12.1 1.5 %collective-permute-start.5 = (bf16[144,2880]{1,0:T(8,128)(2,1)}, bf16[144,2880]{1,0:T(8,128)(2,1)S(1)}, u32[]{:S(2)}, u32[]{:S(2)}) collective-permute-start(bf16[144,2880]{1,0:T(8,128)(2,1)} %split_rows.2), channel_id=1, source_target_pairs={{0,4},{4,0},{8,12},{12,8},{16,20},{20,16},{24,28},{28,24},{1,5},{5... | collective-permute-start | bytes 2488328 | tf_op jit(solution)/shard_map/ppermute | solution.py:377
  13.6 7.4 %split_rows.3 = (bf16[144,2880]{1,0:T(8,128)(2,1)}, bf16[144,2880]{1,0:T(8,128)(2,1)}, bf16[144,2880]{1,0:T(8,128)(2,1)}, bf16[144,2880]{1,0:T(8,128)(2,1)}, bf1...) custom-call(bf16[1152,2880]{1,0:T(8,128)(2,1)} %bitcast.22), custom_call_target="tpu_custom_call" | custom-call | flops 743178240 | bytes 9953280 | tf_op jit(solution)/shard_map/split_rows/pallas_call | solution.py:57
  21.5 5.5 %collective-permute-start.8 = (bf16[144,2880]{1,0:T(8,128)(2,1)}, bf16[144,2880]{1,0:T(8,128)(2,1)}, u32[]{:S(2)}, u32[]{:S(2)}) collective-permute-start(bf16[144,2880]{1,0:T(8,128)(2,1)} %get-tuple-element.33.refs_3_), channel_id=1, source_target_pairs={{0,8},{4,12},{24,16},{28,20},{1,9},{5,13},{25,17},{29,21},{2,10},{... | collective-permute-start | bytes 2488328 | tf_op jit(solution)/shard_map/ppermute | solution.py:381
  27.0 4.2 %collective-permute-done.refs_0_.refs_1_ = bf16[192,2880]{1,0:T(8,128)(2,1)S(1)} collective-permute-done((bf16[192,2880]{1,0:T(8,128)(2,1)}, bf16[192,2880]{1,0:T(8,128)(2,1)S(1)}, u32[]{:S(2)}, u32[]{:S(2)}) %collective-permute-start) | collective-permute-done | bytes 1105952 | tf_op jit(solution)/shard_map/ppermute | solution.py:381
  31.2 1.7 %collective-permute-start.1 = (bf16[192,2880]{1,0:T(8,128)(2,1)S(1)}, bf16[192,2880]{1,0:T(8,128)(2,1)}, u32[]{:S(2)}, u32[]{:S(2)}) collective-permute-start(bf16[192,2880]{1,0:T(8,128)(2,1)S(1)} %collective-permute-done.refs_0_.refs_1_), channel_id=1, source_target_pairs={{8,16},{12,20},{16,24},{20,28},{9,17},{13,21},{17,25},{21,29},{10,... | collective-permute-start | bytes 3317768 | tf_op jit(solution)/shard_map/ppermute | solution.py:381
  35.4 1.6 %slot_marks.1 = s32[8,8,4,192]{3,2,1,0:T(4,128)} custom-call(s32[4,192]{1,0:T(4,128)} %bitcast.25), custom_call_target="tpu_custom_call" | custom-call | flops 2359296 | bytes 196608 | tf_op jit(solution)/shard_map/slot_marks/pallas_call | solution.py:88
  37.0 8.1 %all-to-all-start = ((s32[8,8,4,192]{3,2,1,0:T(4,128)}), s32[8,8,4,192]{3,2,1,0:T(4,128)S(1)}, u32[]{:S(2)}, u32[]{:S(2)}) async-start(s32[8,8,4,192]{3,2,1,0:T(4,128)} %slot_marks.1), calls=%async_computation | async-start | bytes 524288 | tf_op jit(solution)/shard_map/all_to_all | solution.py:369
  45.2 4.8 %collective-permute-start.6 = (bf16[144,2880]{1,0:T(8,128)(2,1)S(1)}, bf16[144,2880]{1,0:T(8,128)(2,1)}, u32[]{:S(2)}, u32[]{:S(2)}) collective-permute-start(bf16[144,2880]{1,0:T(8,128)(2,1)S(1)} %collective-permute-done.5.refs_4_), channel_id=1, source_target_pairs={{0,8},{4,12},{24,16},{28,20},{1,9},{5,13},{25,17},{29,21},{2,10},{... | collective-permute-start | bytes 2488328 | tf_op jit(solution)/shard_map/ppermute | solution.py:381
  50.0 19.4 %all-to-all-done.refs_2_.refs_7_.refs_8_.marks_ref = s32[8,8,4,192]{3,2,1,0:T(4,128)S(1)} async-done(((s32[8,8,4,192]{3,2,1,0:T(4,128)}), s32[8,8,4,192]{3,2,1,0:T(4,128)S(1)}, u32[]{:S(2)}, u32[]{:S(2)}) %all-to-all-start) | async-done | bytes 196640 | tf_op jit(solution)/shard_map/all_to_all | solution.py:369
  70.1 3.1 %pack_rows.1 = (bf16[112,2880]{1,0:T(8,128)(2,1)}, bf16[112,2880]{1,0:T(8,128)(2,1)}) custom-call(bf16[144,2880]{1,0:T(8,128)(2,1)} %get-tuple-element.26.refs_0_, bf16[144,2880]{1,0:T(8,128)(2,1)} %get-tuple-element.27.refs_1_, s32[8,8,4,192]{3,2,1,0:T(4,128)} %copy-done), custom_call_target="tpu_custom_call" | custom-call | flops 185794560 | bytes 3317760 | tf_op jit(solution)/shard_map/pack_rows/pallas_call | solution.py:154
  77.0 3.2 %all-to-all-start.2 = ((f32[4,1,32]{2,1,0:T(1,128)}), f32[4,1,32]{2,1,0:T(1,128)S(1)}, u32[]{:S(2)}, u32[]{:S(2)}) async-start(f32[4,1,32]{2,1,0:T(1,128)} %broadcast_in_dim.24), calls=%async_computation.2 | async-start | bytes 4096 | tf_op jit(solution)/shard_map/all_to_all | solution.py:371
  80.8 4.2 %meet.3.refs_9_ = f32[4,8,192]{2,1,0:T(8,128)} custom-call(bf16[192,2880]{1,0:T(8,128)(2,1)} %copy-done.1, bf16[192,2880]{1,0:T(8,128)(2,1)} %block_ref.1, bf16[192,2880]{1,0:T(8,128)(2,1)} %copy-done.2, bf16[144,2880]{1,0:T(8,128)(2,1)} %get-tuple-element.33.refs_3_, bf16[144,2880]{1,0:T(8,128)(2,1)} %copy-done.3, ...), custom_call_target="tpu_custom_call", output_to_operand_aliasing={{}: (8, {})} | custom-call | flops 637009920 | bytes 6635520 | tf_op jit(solution)/shard_map/meet/pallas_call | solution.py:248
  85.7 4.0 %meet.4 = (f32[4,8,192]{2,1,0:T(8,128)}, f32[1,8,192]{2,1,0:T(8,128)}) custom-call(bf16[192,2880]{1,0:T(8,128)(2,1)} %collective-permute-done.1.refs_0_, bf16[192,2880]{1,0:T(8,128)(2,1)} %copy-done.1, bf16[192,2880]{1,0:T(8,128)(2,1)} %block_ref.1, bf16[192,2880]{1,0:T(8,128)(2,1)} %copy-done.2, ...), custom_call_target="tpu_custom_call", output_to_operand_aliasing={{0}: (9, {}), {1}: (10, {})} | custom-call | flops 477757440 | bytes 4976640 | tf_op jit(solution)/shard_map/meet/pallas_call | solution.py:248
  91.2 3.6 %meet.5 = (f32[4,8,192]{2,1,0:T(8,128)}, f32[1,8,192]{2,1,0:T(8,128)}) custom-call(bf16[192,2880]{1,0:T(8,128)(2,1)} %collective-permute-done.1.refs_0_, bf16[192,2880]{1,0:T(8,128)(2,1)} %copy-done.1, bf16[192,2880]{1,0:T(8,128)(2,1)} %block_ref.1, bf16[192,2880]{1,0:T(8,128)(2,1)} %copy-done.2, ...), custom_call_target="tpu_custom_call", output_to_operand_aliasing={{0}: (8, {}), {1}: (9, {})} | custom-call | flops 318504960 | bytes 3317760 | tf_op jit(solution)/shard_map/meet/pallas_call | solution.py:248
  94.8 3.9 %all-to-all-start.1 = ((f32[4,8,192]{2,1,0:T(8,128)}), f32[4,8,192]{2,1,0:T(8,128)S(1)}, u32[]{:S(2)}, u32[]{:S(2)}) async-start(f32[4,8,192]{2,1,0:T(8,128)} %get-tuple-element.38), calls=%async_computation.1 | async-start | bytes 65536 | tf_op jit(solution)/shard_map/all_to_all | solution.py:428
  101.5 2.4 %router.1 = (f32[32,192]{1,0:T(8,128)}, f32[32,192]{1,0:T(8,128)}, f32[1,32]{1,0:T(1,128)}) custom-call(bf16[32,2880]{1,0:T(8,128)(2,1)} %bitcast.23, bf16[192,2880]{1,0:T(8,128)(2,1)} %tokens_ref.1, f32[32,1]{1,0:T(8,128)} %copy.17.bias_ref, s32[8,4,192]{2,1,0:T(4,128)} %slice_bitcast_fusion.marks_ref), custom_call_target="tpu_custom_call" | custom-call | flops 35389440 | bytes 1290240 | tf_op jit(solution)/shard_map/router/pallas_call | solution.py:115
  105.2 2.6 %last_dots.1.late_ref = f32[4,192]{1,0:T(4,128)} custom-call(bf16[192,2880]{1,0:T(8,128)(2,1)} %block_ref.1, bf16[1,112,2880]{2,1,0:T(8,128)(2,1)} %bitcast.4.rows_ref, s32[8,8,4,192]{3,2,1,0:T(4,128)} %copy-done), custom_call_target="tpu_custom_call" | custom-call | flops 123863040 | bytes 1751040 | tf_op jit(solution)/shard_map/last_dots/pallas_call | solution.py:279
  107.9 2.5 %collective-permute-done.9.guest_ref = f32[1,8,192]{2,1,0:T(8,128)S(1)} collective-permute-done((f32[1,8,192]{2,1,0:T(8,128)S(1)}, f32[1,8,192]{2,1,0:T(8,128)S(1)}, u32[]{:S(2)}, u32[]{:S(2)}) %collective-permute-start.9) | collective-permute-done | bytes 6176 | tf_op jit(solution)/shard_map/ppermute | solution.py:381
  111.0 2.6 %finish.1 = (bf16[32,192]{1,0:T(8,128)(2,1)}, f32[32,4,768]{2,1,0:T(4,128)}) custom-call(f32[1]{0:T(128)S(6)} %copy.23.scale_ref, f32[4,8,192]{2,1,0:T(8,128)} %copy-done.5, f32[1,8,192]{2,1,0:T(8,128)} %copy-done.9, f32[4,192]{1,0:T(4,128)} %last_dots.1.late_ref, f32[32,192]{1,0:T(8,128)} %get-tuple-element.42.mix_ref, ...), custom_call_target="tpu_custom_call" | custom-call | flops 35389440 | bytes 1474560 | tf_op jit(solution)/shard_map/finish/pallas_call | solution.py:331
  113.6 5.7 %all-to-all-start.3 = ((f32[32,4,768]{2,1,0:T(4,128)}), f32[32,4,768]{2,1,0:T(4,128)S(1)}, u32[]{:S(2)}, u32[]{:S(2)}) async-start(f32[32,4,768]{2,1,0:T(4,128)} %get-tuple-element.46), calls=%async_computation.3 | async-start | bytes 786432 | tf_op jit(solution)/shard_map/all_to_all | solution.py:439
  119.4 2.2 %convolution_convert_fusion = bf16[192,2880]{1,0:T(8,128)(2,1)} fusion(bf16[32,192]{1,0:T(8,128)(2,1)} %get-tuple-element.45, bf16[2880,32]{0,1:T(8,128)(2,1)S(1)} %copy-done.4), kind=kOutput, calls=%fused_computation | convolution fusion | flops 35942400 | bytes 1302528 | tf_op jit(solution)/shard_map/dot_general | solution.py:436
  121.5 11.0 %all-to-all-done.3 = f32[32,4,768]{2,1,0:T(4,128)S(1)} async-done(((f32[32,4,768]{2,1,0:T(4,128)}), f32[32,4,768]{2,1,0:T(4,128)S(1)}, u32[]{:S(2)}, u32[]{:S(2)}) %all-to-all-start.3) | async-done | bytes 393248 | tf_op jit(solution)/shard_map/all_to_all | solution.py:439
  (50 shorter events, 16.9 us)
Async XLA Ops:
  0.6 30.6 %collective-permute-start = (bf16[192,2880]{1,0:T(8,128)(2,1)}, bf16[192,2880]{1,0:T(8,128)(2,1)S(1)}, u32[]{:S(2)}, u32[]{:S(2)}) collective-permute-start(bf16[192,2880]{1,0:T(8,128)(2,1)} %block_ref.1), channel_id=1, source_target_pairs={{0,8},{4,12},{8,16},{12,20},{16,24},{20,28},{1,9},{5,13},{9,17},{1... | collective-permute-start | bytes 3317768 | tf_op jit(solution)/shard_map/ppermute | solution.py:381
  5.7 28.5 %collective-permute-start.2 = (bf16[192,2880]{1,0:T(8,128)(2,1)}, bf16[192,2880]{1,0:T(8,128)(2,1)S(1)}, u32[]{:S(2)}, u32[]{:S(2)}) collective-permute-start(bf16[192,2880]{1,0:T(8,128)(2,1)} %block_ref.1), channel_id=1, source_target_pairs={{8,0},{12,4},{16,8},{20,12},{24,16},{28,20},{9,1},{13,5},{17,9},{2... | collective-permute-start | bytes 3317768 | tf_op jit(solution)/shard_map/ppermute | solution.py:381
  12.1 33.0 %collective-permute-start.5 = (bf16[144,2880]{1,0:T(8,128)(2,1)}, bf16[144,2880]{1,0:T(8,128)(2,1)S(1)}, u32[]{:S(2)}, u32[]{:S(2)}) collective-permute-start(bf16[144,2880]{1,0:T(8,128)(2,1)} %split_rows.2), channel_id=1, source_target_pairs={{0,4},{4,0},{8,12},{12,8},{16,20},{20,16},{24,28},{28,24},{1,5},{5... | collective-permute-start | bytes 2488328 | tf_op jit(solution)/shard_map/ppermute | solution.py:377
  21.0 52.2 %collective-permute-start.7 = (bf16[144,2880]{1,0:T(8,128)(2,1)}, bf16[144,2880]{1,0:T(8,128)(2,1)}, u32[]{:S(2)}, u32[]{:S(2)}) collective-permute-start(bf16[144,2880]{1,0:T(8,128)(2,1)} %get-tuple-element.28), channel_id=1, source_target_pairs={{0,4},{4,0},{8,12},{12,8},{16,20},{20,16},{24,28},{28,24},{1,5},{5... | collective-permute-start | bytes 2488328 | tf_op jit(solution)/shard_map/ppermute | solution.py:377
  21.5 53.2 %collective-permute-start.8 = (bf16[144,2880]{1,0:T(8,128)(2,1)}, bf16[144,2880]{1,0:T(8,128)(2,1)}, u32[]{:S(2)}, u32[]{:S(2)}) collective-permute-start(bf16[144,2880]{1,0:T(8,128)(2,1)} %get-tuple-element.33.refs_3_), channel_id=1, source_target_pairs={{0,8},{4,12},{24,16},{28,20},{1,9},{5,13},{25,17},{29,21},{2,10},{... | collective-permute-start | bytes 2488328 | tf_op jit(solution)/shard_map/ppermute | solution.py:381
  31.2 49.6 %copy-start.1 = (bf16[192,2880]{1,0:T(8,128)(2,1)}, bf16[192,2880]{1,0:T(8,128)(2,1)S(1)}, u32[]{:S(2)}) copy-start(bf16[192,2880]{1,0:T(8,128)(2,1)S(1)} %collective-permute-done.refs_0_.refs_1_) | copy-start | bytes 3317764
  31.2 53.9 %collective-permute-start.1 = (bf16[192,2880]{1,0:T(8,128)(2,1)S(1)}, bf16[192,2880]{1,0:T(8,128)(2,1)}, u32[]{:S(2)}, u32[]{:S(2)}) collective-permute-start(bf16[192,2880]{1,0:T(8,128)(2,1)S(1)} %collective-permute-done.refs_0_.refs_1_), channel_id=1, source_target_pairs={{8,16},{12,20},{16,24},{20,28},{9,17},{13,21},{17,25},{21,29},{10,... | collective-permute-start | bytes 3317768 | tf_op jit(solution)/shard_map/ppermute | solution.py:381
  34.1 46.7 %copy-start.2 = (bf16[192,2880]{1,0:T(8,128)(2,1)}, bf16[192,2880]{1,0:T(8,128)(2,1)S(1)}, u32[]{:S(2)}) copy-start(bf16[192,2880]{1,0:T(8,128)(2,1)S(1)} %collective-permute-done.2.refs_2_.refs_3_) | copy-start | bytes 3317764
  34.1 50.9 %collective-permute-start.3 = (bf16[192,2880]{1,0:T(8,128)(2,1)S(1)}, bf16[192,2880]{1,0:T(8,128)(2,1)}, u32[]{:S(2)}, u32[]{:S(2)}) collective-permute-start(bf16[192,2880]{1,0:T(8,128)(2,1)S(1)} %collective-permute-done.2.refs_2_.refs_3_), channel_id=1, source_target_pairs={{8,0},{12,4},{16,8},{20,12},{9,1},{13,5},{17,9},{21,13},{10,2},{14... | collective-permute-start | bytes 3317768 | tf_op jit(solution)/shard_map/ppermute | solution.py:381
  37.0 32.4 %all-to-all-start = ((s32[8,8,4,192]{3,2,1,0:T(4,128)}), s32[8,8,4,192]{3,2,1,0:T(4,128)S(1)}, u32[]{:S(2)}, u32[]{:S(2)}) async-start(s32[8,8,4,192]{3,2,1,0:T(4,128)} %slot_marks.1), calls=%async_computation | async-start | bytes 524288 | tf_op jit(solution)/shard_map/all_to_all | solution.py:369
  45.1 35.7 %copy-start.3 = (bf16[144,2880]{1,0:T(8,128)(2,1)}, bf16[144,2880]{1,0:T(8,128)(2,1)S(1)}, u32[]{:S(2)}) copy-start(bf16[144,2880]{1,0:T(8,128)(2,1)S(1)} %collective-permute-done.5.refs_4_) | copy-start | bytes 2488324
  45.2 46.0 %collective-permute-start.6 = (bf16[144,2880]{1,0:T(8,128)(2,1)S(1)}, bf16[144,2880]{1,0:T(8,128)(2,1)}, u32[]{:S(2)}, u32[]{:S(2)}) collective-permute-start(bf16[144,2880]{1,0:T(8,128)(2,1)S(1)} %collective-permute-done.5.refs_4_), channel_id=1, source_target_pairs={{0,8},{4,12},{24,16},{28,20},{1,9},{5,13},{25,17},{29,21},{2,10},{... | collective-permute-start | bytes 2488328 | tf_op jit(solution)/shard_map/ppermute | solution.py:381
  69.4 0.7 copy-start
  73.2 18.0 %collective-permute-start.4 = (bf16[112,2880]{1,0:T(8,128)(2,1)}, bf16[112,2880]{1,0:T(8,128)(2,1)}, u32[]{:S(2)}, u32[]{:S(2)}) collective-permute-start(bf16[112,2880]{1,0:T(8,128)(2,1)} %get-tuple-element.30), channel_id=1, source_target_pairs={{0,4},{4,0},{8,12},{12,8},{16,20},{20,16},{24,28},{28,24},{1,5},{5... | collective-permute-start | bytes 1935368 | tf_op jit(solution)/shard_map/ppermute | solution.py:377
  74.7 30.5 %collective-permute-start.10 = (bf16[112,2880]{1,0:T(8,128)(2,1)}, bf16[112,2880]{1,0:T(8,128)(2,1)}, u32[]{:S(2)}, u32[]{:S(2)}) collective-permute-start(bf16[112,2880]{1,0:T(8,128)(2,1)} %get-tuple-element.40), channel_id=1, source_target_pairs={{0,4},{4,0},{8,12},{12,8},{16,20},{20,16},{24,28},{28,24},{1,5},{5... | collective-permute-start | bytes 1935368 | tf_op jit(solution)/shard_map/ppermute | solution.py:377
  77.0 17.8 %all-to-all-start.2 = ((f32[4,1,32]{2,1,0:T(1,128)}), f32[4,1,32]{2,1,0:T(1,128)S(1)}, u32[]{:S(2)}, u32[]{:S(2)}) async-start(f32[4,1,32]{2,1,0:T(1,128)} %broadcast_in_dim.24), calls=%async_computation.2 | async-start | bytes 4096 | tf_op jit(solution)/shard_map/all_to_all | solution.py:371
  91.2 9.0 %copy-start.10 = (f32[32]{0:T(128)S(1)}, f32[32]{0:T(128)}, u32[]{:S(2)}) copy-start(f32[32]{0:T(128)} %param.12) | copy-start | bytes 388
  94.8 9.1 %copy-start.6 = (f32[1,8,192]{2,1,0:T(8,128)S(1)}, f32[1,8,192]{2,1,0:T(8,128)}, u32[]{:S(2)}) copy-start(f32[1,8,192]{2,1,0:T(8,128)} %get-tuple-element.39) | copy-start | bytes 18436
  94.8 13.0 %copy-start.7 = (f32[4,1,32]{2,1,0:T(1,128)}, f32[4,1,32]{2,1,0:T(1,128)S(1)}, u32[]{:S(2)}) copy-start(f32[4,1,32]{2,1,0:T(1,128)S(1)} %all-to-all-done.2) | copy-start | bytes 1540
  94.8 15.5 %all-to-all-start.1 = ((f32[4,8,192]{2,1,0:T(8,128)}), f32[4,8,192]{2,1,0:T(8,128)S(1)}, u32[]{:S(2)}, u32[]{:S(2)}) async-start(f32[4,8,192]{2,1,0:T(8,128)} %get-tuple-element.38), calls=%async_computation.1 | async-start | bytes 65536 | tf_op jit(solution)/shard_map/all_to_all | solution.py:428
  103.9 6.4 %collective-permute-start.9 = (f32[1,8,192]{2,1,0:T(8,128)S(1)}, f32[1,8,192]{2,1,0:T(8,128)S(1)}, u32[]{:S(2)}, u32[]{:S(2)}) collective-permute-start(f32[1,8,192]{2,1,0:T(8,128)S(1)} %copy-done.6), channel_id=1, source_target_pairs={{8,24},{12,28},{16,0},{20,4},{9,25},{13,29},{17,1},{21,5},{10,26},... | collective-permute-start | bytes 18440 | tf_op jit(solution)/shard_map/ppermute | solution.py:381
  107.9 11.5 %copy-start.4 = (bf16[2880,32]{0,1:T(8,128)(2,1)S(1)}, bf16[2880,32]{0,1:T(8,128)(2,1)}, u32[]{:S(2)}) copy-start(bf16[2880,32]{0,1:T(8,128)(2,1)} %param.11) | copy-start | bytes 552964
  110.4 9.0 %copy-start.8 = (f32[4,1,32]{2,1,0:T(1,128)S(1)}, f32[4,1,32]{2,1,0:T(1,128)}, u32[]{:S(2)}) copy-start(f32[4,1,32]{2,1,0:T(1,128)} %copy-done.7) | copy-start | bytes 1540
  113.6 19.0 %all-to-all-start.3 = ((f32[32,4,768]{2,1,0:T(4,128)}), f32[32,4,768]{2,1,0:T(4,128)S(1)}, u32[]{:S(2)}, u32[]{:S(2)}) async-start(f32[32,4,768]{2,1,0:T(4,128)} %get-tuple-element.46), calls=%async_computation.3 | async-start | bytes 786432 | tf_op jit(solution)/shard_map/all_to_all | solution.py:439
  (2 other events, 1.2 us)
